TPU v7x, 128 devices: a whole 4x4x4 slice. The times are simulated.
128 devices in a mesh: grp: 4 (over x), dp: 32 (over y, z, core).
Axes of the slice: x: 4, y: 4, z: 4, core: 2. Of those that a mesh axis runs over, the one named last changes fastest.
Arguments:
- inputs: bfloat16 [49152, 2048], P(('grp', 'dp')), may hold values from -6 to 6
- upstream: bfloat16 [49152, 2048], P(('grp', 'dp')), may hold values from -18 to 18
- doc_ids: int32 [49152], P(('grp', 'dp')), may hold values from 0 to 1023, never falling along the last dimension, each value on 1 to 128 neighbouring positions
- qkv_weight: float32 [2048, 3072], P(('grp', 'dp')), may hold values from -8 to 8
- out_weight: float32 [2048, 2048], P(('grp', 'dp')), may hold values from -0.125 to 0.125
- qkv_mean: float32 [2048, 3072], P(('grp', 'dp')), may hold values from -3 to 3
- qkv_square: float32 [2048, 3072], P(('grp', 'dp')), may hold values from 0.3 to 3
- out_mean: float32 [2048, 2048], P(('grp', 'dp')), may hold values from -3 to 3
- out_square: float32 [2048, 2048], P(('grp', 'dp')), may hold values from 0.3 to 3
Outputs:
- attn_out: bfloat16 [49152, 2048], P(('grp', 'dp'))
- new_qkv_weight: float32 [2048, 3072], P(('grp', 'dp'))
- new_out_weight: float32 [2048, 2048], P(('grp', 'dp'))
- new_qkv_mean: float32 [2048, 3072], P(('grp', 'dp'))
- new_qkv_square: float32 [2048, 3072], P(('grp', 'dp'))
- new_out_mean: float32 [2048, 2048], P(('grp', 'dp'))
- new_out_square: float32 [2048, 2048], P(('grp', 'dp'))
All inputs are finite; a program needn't handle non-finite values.
Results may differ from a plain program's by a relative error of at most 0.0075.
The roundings to bfloat16 on the way count: a program that leaves them out, or rounds other values in their place, can miss the bound.
Values may be sent and summed in bfloat16 or wider, within the bound.
No kernel may reach another device: no remote copies, remote signals or barrier semaphores. Data moves between devices by JAX's collectives and lax.ppermute only.
A program may use at most 128 MiB of HBM per device.

v0:
```python
import math

import jax
import jax.numpy as jnp
import numpy as np
from jax import lax
from jax.experimental import pallas as pl
from jax.experimental.pallas import tpu as pltpu
from jax.sharding import Mesh
from jax.sharding import PartitionSpec as P


HD = 128
TOK = 384
ALL = ("grp", "dp_0", "dp_1", "dp_2")

beta_one = 0.9
beta_two = 0.95
learn_rate = 0.0003
decay_rate = 0.1
epsilon = 1e-08
step_count = 10
norm_eps = 1e-05
masked_score = -1e30
scale = HD ** (-0.5)


MASKS = [(1 if d % 2 == 0 else 3) << (2 * (2 - d // 2)) for d in range(6)]
LATE = ((0, 2, 4), (1, 3, 5))
EARLY = ((1, 3, 5), (0, 2, 4))


def late_links(rotation, stage):
    return tuple(MASKS[LATE[c][(rotation + stage) % 3]] for c in range(2))


def early_mask(core, p):
    m = 0
    for bit in range(3):
        if p >> bit & 1:
            m ^= MASKS[EARLY[core][bit]]
    return m


def block_masks():
    table = np.zeros((2, 3, 64), np.int32)
    for c in range(2):
        for rotation in range(3):
            for p in range(64):
                m = early_mask(c, p)
                for bit in range(3):
                    if p >> (3 + bit) & 1:
                        m ^= MASKS[LATE[c][(rotation + bit) % 3]]
                table[c, rotation, p] = m
    return table


TABLE = block_masks()


def across(x, masks):
    pairs = [((t * 2 + c), ((t ^ masks[c]) * 2 + c)) for t in range(64) for c in range(2)]
    return lax.ppermute(x, ALL, pairs)


def early(x, p):
    return across(x, [early_mask(c, p) for c in range(2)])


def to_partner(x):
    return lax.ppermute(x, "dp_2", [(0, 1), (1, 0)])


def out_pairs():
    pairs = []
    for chip in range(64):
        for c in range(2):
            x = chip >> 4
            target = ((x % 2) * 2 + c) * 16 + (chip & 15)
            pairs.append((chip * 2 + c, target * 2 + x // 2))
    return pairs


def out_row(t):
    xp = t >> 4
    return ((xp >> 1) * 16 + (t & 15)) * 2 + (xp & 1)


def normalize(rows_in):
    values = rows_in.astype(jnp.float32)
    factor = lax.rsqrt(jnp.mean(values * values, axis=-1, keepdims=True) + norm_eps)
    return (values * factor).astype(jnp.bfloat16)


ANY = pl.BlockSpec(memory_space=pl.ANY)
HBM = pl.BlockSpec(memory_space=pltpu.HBM)
SMEM = pl.BlockSpec(memory_space=pltpu.SMEM)
VMEM = pl.BlockSpec(memory_space=pltpu.VMEM)
BF = jnp.bfloat16
F32 = jnp.float32


def cost(flops, nbytes):
    return pl.CostEstimate(flops=flops, bytes_accessed=nbytes, transcendentals=0)


def place_stream(ids, rotation, a, b, w, sem):
    def step(p, carry):
        pltpu.make_async_copy(a.at[p], w.at[ids[rotation, p]], sem).start()
        pltpu.make_async_copy(b.at[p], w.at[ids[rotation, p + 32]], sem).start()
        return carry

    lax.fori_loop(0, 32, step, 0, unroll=8)


def nn(a, b):
    return jnp.dot(a, b, preferred_element_type=F32)


def nt(a, b):
    return lax.dot_general(a, b, (((1,), (1,)), ((), ())), preferred_element_type=F32)


def tn(a, b):
    return lax.dot_general(a, b, (((0,), (0,)), ((), ())), preferred_element_type=F32)


def stacked(ref, g, rows):
    return jnp.concatenate([ref[g, rows, HD * h : HD * (h + 1)] for h in range(4)], axis=0)


def softmax_block(q_ref, kv_ref, col_ref, row_ref, g, seq, i):
    lo, hi = max(0, 128 * (i - 1)), 128 * (i + 1)
    n = hi - lo
    base = seq * TOK
    rows = pl.ds(pl.multiple_of(base + 128 * i, 128), 128)
    keys = pl.ds(pl.multiple_of(base + lo, 128), n)
    q = stacked(q_ref, g, rows)
    scores = nt(q, kv_ref[g, keys, :]) * scale
    t = lax.broadcasted_iota(jnp.int32, (128, n), 0) + 128 * i
    s = lax.broadcasted_iota(jnp.int32, (128, n), 1) + lo
    allowed = (t >= s) & (col_ref[rows, :] == row_ref[seq, :, lo:hi])
    scores = jnp.where(allowed[None], scores.reshape(4, 128, n), masked_score).reshape(512, n)
    exponent = jnp.exp(scores - jnp.max(scores, axis=-1, keepdims=True))
    soft = exponent * (1.0 / jnp.sum(exponent, axis=-1, keepdims=True))
    return q, soft, rows, keys


def load_rows(own, other, dst, sem):
    pltpu.make_async_copy(own, dst.at[pl.ds(0, TOK)], sem).start()
    pltpu.make_async_copy(other, dst.at[pl.ds(TOK, TOK)], sem).start()


def wait_all(ref, sem):
    pltpu.make_async_copy(ref, ref, sem).wait()


def spread_out_rows(ids, half, g, keep, send, sem):
    def step(p, carry):
        pltpu.make_async_copy(g.at[half, ids[3 + half, p + 32]], send.at[p], sem).start()
        pltpu.make_async_copy(g.at[half, ids[3 + half, p]], keep.at[p], sem).start()
        return carry

    lax.fori_loop(0, 32, step, 0, unroll=8)


def project_body(*refs):
    ids, xa, xb, ua, ub, a0, b0, a1, b1, a2, b2, col_ref, row_ref = refs[:13]
    q_out, kv_out, o_out, keep3, send3, keep4, send4 = refs[13:20]
    x, u, w, rows_out, kv_ref, o_ref, g, sems = refs[20:]
    q_ref = rows_out
    pairs = ((a0, b0), (a1, b1), (a2, b2))
    load_rows(xa, xb, x, sems.at[3])
    for s in range(3):
        place_stream(ids, s, *pairs[s], w.at[s], sems.at[s])
    load_rows(ua, ub, u, sems.at[4])
    wait_all(x, sems.at[3])

    def column(s, carry):
        wait_all(w.at[s], sems.at[s])
        rows_out[s] = nn(x[...], w[s].reshape(2048, 512)).astype(BF)
        return carry

    lax.fori_loop(0, 3, column, 0)
    for j in range(4):
        kv_ref[j] = rows_out[2, :, HD * j : HD * (j + 1)]
    copies = [
        pltpu.make_async_copy(a, b, sems.at[7 + i])
        for i, (a, b) in enumerate(
            ((rows_out.at[pl.ds(0, 2)], q_out), (kv_ref, kv_out), (o_ref, o_out))
        )
    ]
    copies[0].start()
    copies[1].start()

    def unit(n, carry):
        h, seq = n // 2, n % 2
        for i in range(3):
            _, soft, rows, keys = softmax_block(q_ref, kv_ref, col_ref, row_ref, h, seq, i)
            mixed = nn(soft.astype(BF), kv_ref[2 + h, keys, :]).astype(BF)
            for j in range(4):
                o_ref[h, rows, HD * j : HD * (j + 1)] = mixed[128 * j : 128 * (j + 1)]
        return carry

    lax.fori_loop(0, 4, unit, 0, unroll=2)
    copies[2].start()
    wait_all(u, sems.at[4])
    for half, keep, send in ((0, keep3, send3), (1, keep4, send4)):

        def group(h, carry):
            out = tn(o_ref[h], u[:, 1024 * half : 1024 * (half + 1)]).astype(BF)
            g[half, pl.ds(32 * h, 32)] = out.reshape(32, 16, 1024)
            return carry

        lax.fori_loop(0, 2, group, 0)
        spread_out_rows(ids, half, g, keep, send, sems.at[5 + half])
    for half in range(2):
        wait_all(g.at[half], sems.at[5 + half])
    for copy in copies:
        copy.wait()


PAIR = jax.ShapeDtypeStruct((2, 2 * TOK, 512), BF)
HALF = jax.ShapeDtypeStruct((32, 32, 512), BF)
WIDE = jax.ShapeDtypeStruct((32, 16, 1024), BF)


ROWS = pltpu.VMEM((2 * TOK, 2048), BF)


def project(ids, x, u, streams, col, row):
    return pl.pallas_call(
        project_body,
        in_specs=[SMEM] + [HBM] * 10 + [VMEM] * 2,
        out_specs=(ANY,) * 7,
        out_shape=(PAIR, jax.ShapeDtypeStruct((4, 2 * TOK, HD), BF), PAIR) + (WIDE,) * 4,
        scratch_shapes=[
            ROWS,
            ROWS,
            pltpu.VMEM((3, 64, 32, 512), BF),
            pltpu.VMEM((3, 2 * TOK, 512), BF),
            pltpu.VMEM((4, 2 * TOK, HD), BF),
            pltpu.VMEM((2, 2 * TOK, 512), BF),
            pltpu.VMEM((2, 64, 16, 1024), BF),
            pltpu.SemaphoreType.DMA((10,)),
        ],
        cost_estimate=cost(2 * 768 * 2048 * 2560, 20 << 20),
        name="project",
    )(ids, *x, *u, *[piece for pair in streams for piece in pair], col, row)


def backward_body(*refs):
    ids, xa, xb, ua, ub, a3, b3, a4, b4, q_ref, kv_ref, col_ref, row_ref = refs[:13]
    w_out, keep0, send0, keep1, send1, keep2, send2 = refs[13:20]
    x, u, w_ref, d_ref, dq, dkv, g, acc, sems = refs[20:]
    load_rows(ua, ub, u, sems.at[0])

    def place(p, carry):
        for half, a, b in ((0, a3, b3), (1, a4, b4)):
            cols = pl.ds(1024 * half, 1024)
            pltpu.make_async_copy(
                a.at[p], w_ref.at[ids[3 + half, p], :, cols], sems.at[1]
            ).start()
            pltpu.make_async_copy(
                b.at[p], w_ref.at[ids[3 + half, p + 32], :, cols], sems.at[1]
            ).start()
        return carry

    lax.fori_loop(0, 32, place, 0, unroll=4)
    load_rows(xa, xb, x, sems.at[2])
    wait_all(u, sems.at[0])
    wait_all(w_ref, sems.at[1])
    w_copy = pltpu.make_async_copy(w_ref, w_out, sems.at[6])
    w_copy.start()

    def heads(h, carry):
        d_ref[h] = nt(u[...], w_ref[pl.ds(32 * h, 32)].reshape(512, 2048)).astype(BF)
        return carry

    lax.fori_loop(0, 2, heads, 0)

    def unit(n, carry):
        h, seq = n // 2, n % 2
        acc[...] = jnp.zeros_like(acc)
        for i in range(3):
            q, soft, rows, keys = softmax_block(q_ref, kv_ref, col_ref, row_ref, h, seq, i)
            own = slice(max(0, 128 * (i - 1)), 128 * (i + 1))
            d_heads = stacked(d_ref, h, rows)
            d_soft = nt(d_heads, kv_ref[2 + h, keys, :])
            delta = jnp.sum(soft * d_soft, axis=-1, keepdims=True)
            d_scores = (soft * (d_soft - delta)).astype(BF)
            acc[1, own, :] += tn(soft.astype(BF), d_heads)
            acc[0, own, :] += tn(d_scores, q)
            d_query = (nn(d_scores, kv_ref[h, keys, :]) * scale).astype(BF)
            for j in range(4):
                dq[h, rows, HD * j : HD * (j + 1)] = d_query[128 * j : 128 * (j + 1)]
        all_rows = pl.ds(pl.multiple_of(seq * TOK, 128), TOK)
        dkv[h, all_rows, :] = (acc[0] * scale).astype(BF)
        dkv[2 + h, all_rows, :] = acc[1].astype(BF)
        return carry

    lax.fori_loop(0, 4, unit, 0)
    for j in range(4):
        dq[2, :, HD * j : HD * (j + 1)] = dkv[j]
    wait_all(x, sems.at[2])

    def grads(s, carry):
        g[s] = tn(x[...], dq[s]).astype(BF).reshape(64, 32, 512)
        for j, keep, send in ((0, keep0, send0), (1, keep1, send1), (2, keep2, send2)):

            @pl.when(s == j)
            def _():
                def step(p, inner):
                    pltpu.make_async_copy(
                        g.at[j, ids[j, p + 32]], send.at[p], sems.at[3 + j]
                    ).start()
                    pltpu.make_async_copy(
                        g.at[j, ids[j, p]], keep.at[p], sems.at[3 + j]
                    ).start()
                    return inner

                lax.fori_loop(0, 32, step, 0, unroll=8)

        return carry

    lax.fori_loop(0, 3, grads, 0)
    for j in range(3):
        wait_all(g.at[j], sems.at[3 + j])
    w_copy.wait()


def backward(ids, x, u, streams, q, kv, col, row):
    return pl.pallas_call(
        backward_body,
        in_specs=[SMEM] + [HBM] * 8 + [VMEM] * 4,
        out_specs=(ANY,) * 7,
        out_shape=(jax.ShapeDtypeStruct((64, 16, 2048), BF),) + (HALF,) * 6,
        scratch_shapes=[
            ROWS,
            ROWS,
            pltpu.VMEM((64, 16, 2048), BF),
            pltpu.VMEM((2, 2 * TOK, 512), BF),
            pltpu.VMEM((3, 2 * TOK, 512), BF),
            pltpu.VMEM((4, 2 * TOK, HD), BF),
            pltpu.VMEM((3, 64, 32, 512), BF),
            pltpu.VMEM((2, TOK, HD), F32),
            pltpu.SemaphoreType.DMA((7,)),
        ],
        cost_estimate=cost(2 * 768 * 2048 * 2560, 20 << 20),
        name="back",
    )(ids, *x, *u, *[piece for pair in streams for piece in pair], q, kv, col, row)


def moved(body, ins, outs):
    def kernel(*refs):
        sem = refs[-1]
        copies = [pltpu.make_async_copy(a, b, sem.at[i]) for i, (a, b) in enumerate(body(*refs[:-1]))]
        for copy in copies:
            copy.start()
        for copy in copies:
            copy.wait()

    return pl.pallas_call(
        kernel,
        in_specs=[HBM] * len(ins),
        out_specs=(VMEM,) * len(outs),
        out_shape=outs,
        scratch_shapes=[pltpu.SemaphoreType.DMA((40,))],
    )(*ins)


def by_stream(pieces):
    def pairs(*refs):
        sources, outs = refs[:4], refs[4:]
        copies = []
        for i, src in enumerate(sources):
            at = pl.ds(2 * i, 2)
            for s in range(3):
                copies.append((src.at[:, pl.ds(32 * s, 32)], outs[s].at[at]))
            for j in range(4):
                target = outs[3 + j // 2].at[at, :, pl.ds(512 * (j % 2), 512)]
                copies.append((src.at[:, pl.ds(96 + 16 * j, 16)], target))
        return copies

    shapes = (jax.ShapeDtypeStruct((8, 32, 512), BF),) * 3
    shapes += (jax.ShapeDtypeStruct((8, 16, 1024), BF),) * 2
    return moved(pairs, pieces, shapes)


def added(a, b):
    return (a.astype(F32) + b.astype(F32)).astype(BF)


def after(x, *deps):
    return lax.optimization_barrier((x, deps))[0]


def late_step(stream, keep, send, stage, *gates):
    recv = across(send, late_links(stream % 3, stage))
    if gates:
        keep = after(keep, *gates)
    n = keep.shape[0] // 2
    if stage == 0:
        return added(keep, recv), None
    return added(keep[:n], recv[:n]), added(keep[n:], recv[n:])


def early_reduce(x):
    total = x[0:2].astype(F32)
    for recv in [early(x[p : p + 2], p) for p in (6, 2, 4)]:
        total = total + recv.astype(F32)
    recv = early(total[1].astype(BF), 1)
    return total[0] + recv.astype(F32)


def adamw(weight, mean_in, square_in, grad):
    new_mean = beta_one * mean_in + (1.0 - beta_one) * grad
    new_square = beta_two * square_in + (1.0 - beta_two) * grad * grad
    corrected = (
        new_mean
        / (1.0 - beta_one**step_count)
        / (jnp.sqrt(new_square / (1.0 - beta_two**step_count)) + epsilon)
    )
    return (weight - learn_rate * (corrected + decay_rate * weight), new_mean, new_square)


def halves(rows):
    return [
        jnp.concatenate(
            [
                rows[:, 1024 * h : 1024 * (h + 1)],
                rows[:, 2048 + 256 * h : 2048 + 256 * (h + 1)],
                rows[:, 2560 + 256 * h : 2560 + 256 * (h + 1)],
            ],
            axis=1,
        )
        for h in range(2)
    ]


def local(
    inputs, upstream, doc_ids, qkv_weight, out_weight, qkv_mean, qkv_square, out_mean, out_square
):
    core = lax.axis_index("dp_2")
    chip = lax.axis_index(("grp", "dp_0", "dp_1"))
    first = core == 0
    ids = jnp.where(first, TABLE[0], TABLE[1]) ^ chip
    ids = jnp.concatenate([ids, out_row(ids[:2])], axis=0)

    h0, h1 = halves(qkv_weight.astype(BF))
    mine, theirs = jnp.where(first, h0, h1), jnp.where(first, h1, h0)
    arrived = to_partner(theirs)
    out_block = lax.ppermute(out_weight.astype(BF), ALL, out_pairs())
    top, bottom = jnp.where(first, mine, arrived), jnp.where(first, arrived, mine)
    block = jnp.concatenate(
        [part[:, 512 * s : 512 * (s + 1)] for s in range(3) for part in (top, bottom)]
        + [out_block[:, 512 * s : 512 * (s + 1)] for s in range(4)],
        axis=0,
    )
    low = jnp.stack([block, early(block, 1)])
    have = list(by_stream([low] + [early(low, p) for p in (2, 4, 6)]))

    def gather(s, stage):
        return across(have[s], late_links(s % 3, stage))

    for stage in range(2):
        recv = [gather(s, stage) for s in range(3)]
        have[:3] = [jnp.concatenate(pair, axis=0) for pair in zip(have[:3], recv)]
    streams = [(have[s], gather(s, 2)) for s in range(3)]

    x = (inputs, to_partner(after(inputs, arrived)))
    u = (upstream, to_partner(after(upstream, arrived)))
    docs = jnp.stack([doc_ids, to_partner(after(doc_ids, arrived))])
    col, row = docs.reshape(2 * TOK, 1), docs.reshape(2, 1, TOK)
    x = tuple(normalize(rows) for rows in x)

    for stage in range(2):
        recv = [gather(s, stage) for s in (3, 4)]
        have[3:] = [jnp.concatenate(pair, axis=0) for pair in zip(have[3:], recv)]
    streams += [(have[s], gather(s, 2)) for s in (3, 4)]

    q, kv, mixed, keep3, send3, keep4, send4 = project(
        ids, after(x, have), u, streams[:3], col, row
    )
    out_half, keep0, send0, keep1, send1, keep2, send2 = backward(
        ids, after(x, send3), u, streams[3:], q, kv, col, row
    )
    keep3, send3 = late_step(3, keep3, send3, 2, send2)
    keep4, send4 = late_step(4, keep4, send4, 2, send2)

    out_half = out_half.reshape(1024, 2048)
    mixed = after(mixed, send2, send3, send4)
    mixed = jnp.concatenate([mixed[0], mixed[1]], axis=1)
    other = jnp.dot(mixed[TOK:], out_half, preferred_element_type=F32)
    keep0, send0 = late_step(0, keep0, send0, 2, other)
    keep1, send1 = late_step(1, keep1, send1, 2, other)
    keep2, send2 = late_step(2, keep2, send2, 2, other)
    keep3, send3 = late_step(3, keep3, send3, 1, send2)
    keep4, send4 = late_step(4, keep4, send4, 1, send2)
    own = jnp.dot(after(mixed[:TOK], send3, send4), out_half, preferred_element_type=F32)
    attn_out = (own + to_partner(other)).astype(BF)
    keep0, send0 = late_step(0, keep0, send0, 1, attn_out)
    keep1, send1 = late_step(1, keep1, send1, 1, attn_out)
    keep2, send2 = late_step(2, keep2, send2, 1, attn_out)
    keep3, _ = late_step(3, keep3, send3, 0, send2)
    keep4, _ = late_step(4, keep4, send4, 0, send2)
    keep0, _ = late_step(0, keep0, send0, 0)
    keep1, _ = late_step(1, keep1, send1, 0)
    keep2, _ = late_step(2, keep2, send2, 0)
    outs = [k[:, :, 512 * j : 512 * (j + 1)] for k in (keep3, keep4) for j in range(2)]
    total = early_reduce(jnp.concatenate([keep0, keep1, keep2] + outs, axis=1))
    qkv_sum, out_sum = total[:96], total[96:]

    squares = jnp.sum((total * total).reshape(160, 4, 128), axis=(0, 1))
    spread = lax.all_to_all(
        jnp.broadcast_to(squares, (128, 128)), ALL, split_axis=0, concat_axis=0, tiled=True
    )
    squares = jnp.sum(spread)
    rows = qkv_sum.reshape(3, 2, 16, 512)
    mine = jnp.where(first, rows[:, 0], rows[:, 1])
    arrived = to_partner(jnp.where(first, rows[:, 1], rows[:, 0]))
    low, high = jnp.where(first, mine, arrived), jnp.where(first, arrived, mine)
    grad_qkv = jnp.concatenate(
        [low[0], low[1], high[0], high[1]]
        + [low[2, :, :256], high[2, :, :256], low[2, :, 256:], high[2, :, 256:]],
        axis=1,
    )
    back = [(b, a) for a, b in out_pairs()]
    out_rows = jnp.concatenate([out_sum[16 * s : 16 * (s + 1)] for s in range(4)], axis=1)
    grad_out = lax.ppermute(out_rows, ALL, back)

    param_count = 2048 * (3072 + 2048)
    clip = jnp.minimum(1.0, math.sqrt(param_count) / (jnp.sqrt(squares) + 1e-06))
    new_qkv_weight, new_qkv_mean, new_qkv_square = adamw(
        qkv_weight, qkv_mean, qkv_square, clip * grad_qkv
    )
    new_out_weight, new_out_mean, new_out_square = adamw(
        out_weight, out_mean, out_square, clip * grad_out
    )
    return (
        attn_out,
        new_qkv_weight,
        new_out_weight,
        new_qkv_mean,
        new_qkv_square,
        new_out_mean,
        new_out_square,
    )


def solution(mesh):
    finer = Mesh(mesh.devices.reshape(4, 4, 4, 2), ALL)
    wide = P(ALL, None)
    return jax.shard_map(
        local,
        mesh=finer,
        in_specs=(wide, wide, P(ALL), wide, wide, wide, wide, wide, wide),
        out_specs=(wide,) * 7,
        check_vma=False,
    )
```

profile of v0, /device:TPU:1, one launch (start us, length us, event | category | flops | bytes accessed | tf_op | source)
XLA Modules:
  0.0 216.4 jit_solution(10040147189851443634)
XLA Ops:
  1.7 4.5 %collective-permute-start.2 = (bf16[16,2048]{1,0:T(8,128)(2,1)S(1)}, bf16[16,2048]{1,0:T(8,128)(2,1)S(1)}, u32[]{:S(2)}, u32[]{:S(2)}) collective-permute-start(bf16[16,2048]{1,0:T(8,128)(2,1)S(1)} %convert_element_type.270), channel_id=1, source_target_pairs={{0,0},{1,32},{2,2},{3,34},{4,4},{5,36},{6,6},{7,38},{8,8},{9,40},{... | collective-permute-start | bytes 196616 | tf_op jit(solution)/shard_map/ppermute | solution.py:453
  7.3 1.8 fusion
  10.7 1.9 collective-permute-start.3
  12.7 2.7 %collective-permute-done.3 = bf16[160,512]{1,0:T(8,128)(2,1)S(1)} collective-permute-done((bf16[160,512]{1,0:T(8,128)(2,1)S(1)}, bf16[160,512]{1,0:T(8,128)(2,1)S(1)}, u32[]{:S(2)}, u32[]{:S(2)}) %collective-permute-start.3) | collective-permute-done | bytes 163872 | tf_op jit(solution)/shard_map/ppermute | solution.py:63
  15.4 2.7 %collective-permute-start.6 = (bf16[2,160,512]{2,1,0:T(8,128)(2,1)S(1)}, bf16[2,160,512]{2,1,0:T(8,128)(2,1)}, u32[]{:S(2)}, u32[]{:S(2)}) collective-permute-start(bf16[2,160,512]{2,1,0:T(8,128)(2,1)S(1)} %pad_maximum_fusion.7.refs_0_), channel_id=1, source_target_pairs={{0,30},{1,11},{2,28},{3,9},{4,26},{5,15},{6,24},{7,13},{8,22},{9,3... | collective-permute-start | bytes 983048 | tf_op jit(solution)/shard_map/ppermute | solution.py:63
  18.5 6.7 %collective-permute-start.21 = (s32[384]{0:T(512)S(1)}, s32[384]{0:T(512)S(1)}, u32[]{:S(2)}, u32[]{:S(2)}) collective-permute-start(s32[384]{0:T(512)S(1)} %copy-done.24), channel_id=1, source_target_pairs={{0,1},{1,0},{2,3},{3,2},{4,5},{5,4},{6,7},{7,6},{8,9},{9,8},{10,11... | collective-permute-start | bytes 4616 | tf_op jit(solution)/shard_map/ppermute | solution.py:71
  28.0 2.7 %shard_map.162 = (bf16[8,32,512]{2,1,0:T(8,128)(2,1)}, bf16[8,32,512]{2,1,0:T(8,128)(2,1)}, bf16[8,32,512]{2,1,0:T(8,128)(2,1)}, bf16[8,16,1024]{2,1,0:T(8,128)(2,1)}, bf16[8,16,1024]{2,1,0:T(8,128)(2,1)}) custom-call(bf16[2,160,512]{2,1,0:T(8,128)(2,1)} %copy-done.2, bf16[2,160,512]{2,1,0:T(8,128)(2,1)} %collective-permute-done.4.refs_1_, ...), custom_call_target="tpu_custom_call" | custom-call | tf_op jit(solution)/shard_map/pallas_call | solution.py:363
  30.8 1.6 collective-permute-start.7
  32.3 2.5 %collective-permute-start.11 = (bf16[8,32,512]{2,1,0:T(8,128)(2,1)}, bf16[8,32,512]{2,1,0:T(8,128)(2,1)S(1)}, u32[]{:S(2)}, u32[]{:S(2)}) collective-permute-start(bf16[8,32,512]{2,1,0:T(8,128)(2,1)} %get-tuple-element.50), channel_id=1, source_target_pairs={{0,2},{1,7},{2,0},{3,5},{4,6},{5,3},{6,4},{7,1},{8,10},{9,15},{10,... | collective-permute-start | bytes 786440 | tf_op jit(solution)/shard_map/ppermute | solution.py:63
  34.9 2.7 %collective-permute-start.15 = (bf16[8,16,1024]{2,1,0:T(8,128)(2,1)}, bf16[8,16,1024]{2,1,0:T(8,128)(2,1)S(1)}, u32[]{:S(2)}, u32[]{:S(2)}) collective-permute-start(bf16[8,16,1024]{2,1,0:T(8,128)(2,1)} %get-tuple-element.52), channel_id=1, source_target_pairs={{0,8},{1,25},{2,10},{3,27},{4,12},{5,29},{6,14},{7,31},{8,0},{9,17... | collective-permute-start | bytes 786440 | tf_op jit(solution)/shard_map/ppermute | solution.py:63
  38.7 1.9 constant_dynamic-update-slice_fusion.21
  41.6 2.7 %collective-permute-start.9 = (bf16[8,32,512]{2,1,0:T(8,128)(2,1)S(1)}, bf16[8,32,512]{2,1,0:T(8,128)(2,1)S(1)}, u32[]{:S(2)}, u32[]{:S(2)}) collective-permute-start(bf16[8,32,512]{2,1,0:T(8,128)(2,1)S(1)} %copy-done.10), channel_id=1, source_target_pairs={{0,8},{1,25},{2,10},{3,27},{4,12},{5,29},{6,14},{7,31},{8,0},{9,17... | collective-permute-start | bytes 786440 | tf_op jit(solution)/shard_map/ppermute | solution.py:63
  45.8 2.2 %collective-permute-done.9 = bf16[8,32,512]{2,1,0:T(8,128)(2,1)S(1)} collective-permute-done((bf16[8,32,512]{2,1,0:T(8,128)(2,1)S(1)}, bf16[8,32,512]{2,1,0:T(8,128)(2,1)S(1)}, u32[]{:S(2)}, u32[]{:S(2)}) %collective-permute-start.9) | collective-permute-done | bytes 262176 | tf_op jit(solution)/shard_map/ppermute | solution.py:63
  49.3 1.6 collective-permute-done.13
  50.9 4.0 %collective-permute-done.8 = bf16[16,32,512]{2,1,0:T(8,128)(2,1)S(1)} collective-permute-done((bf16[16,32,512]{2,1,0:T(8,128)(2,1)S(1)}, bf16[16,32,512]{2,1,0:T(8,128)(2,1)S(1)}, u32[]{:S(2)}, u32[]{:S(2)}) %collective-permute-start.8) | collective-permute-done | bytes 524320 | tf_op jit(solution)/shard_map/ppermute | solution.py:63
  58.2 1.9 collective-permute-done.10
  61.3 2.9 %collective-permute-done.14 = bf16[16,16,1024]{2,1,0:T(8,128)(2,1)S(1)} collective-permute-done((bf16[16,16,1024]{2,1,0:T(8,128)(2,1)S(1)}, bf16[16,16,1024]{2,1,0:T(8,128)(2,1)S(1)}, u32[]{:S(2)}, u32[]{:S(2)}) %collective-permute-start.14) | collective-permute-done | bytes 524320 | tf_op jit(solution)/shard_map/ppermute | solution.py:63
  64.2 1.5 collective-permute-start.19
  69.1 2.9 %collective-permute-start.22 = (bf16[32,16,1024]{2,1,0:T(8,128)(2,1)}, bf16[32,16,1024]{2,1,0:T(8,128)(2,1)}, u32[]{:S(2)}, u32[]{:S(2)}) collective-permute-start(bf16[32,16,1024]{2,1,0:T(8,128)(2,1)} %constant_dynamic-update-slice_fusion.19.refs_5_), channel_id=1, source_target_pairs={{0,2},{1,7},{2,0},{3,5},{4,6},{5,3},{6,4},{7,1},{8,10},{9,15},{10,... | collective-permute-start | bytes 3145736 | tf_op jit(solution)/shard_map/ppermute | solution.py:63
  72.0 1.5 fusion.3.refs_2_
  73.5 1.9 collective-permute-done.20.refs_10_
  75.4 3.6 %collective-permute-done.19.refs_8_ = bf16[32,32,512]{2,1,0:T(8,128)(2,1)S(1)} collective-permute-done((bf16[32,32,512]{2,1,0:T(8,128)(2,1)S(1)}, bf16[32,32,512]{2,1,0:T(8,128)(2,1)S(1)}, u32[]{:S(2)}, u32[]{:S(2)}) %collective-permute-start.19) | collective-permute-done | bytes 1048608 | tf_op jit(solution)/shard_map/ppermute | solution.py:63
  79.1 2.4 %collective-permute-done.18.refs_6_ = bf16[32,32,512]{2,1,0:T(8,128)(2,1)S(1)} collective-permute-done((bf16[32,32,512]{2,1,0:T(8,128)(2,1)S(1)}, bf16[32,32,512]{2,1,0:T(8,128)(2,1)S(1)}, u32[]{:S(2)}, u32[]{:S(2)}) %collective-permute-start.18) | collective-permute-done | bytes 1048608 | tf_op jit(solution)/shard_map/ppermute | solution.py:63
  82.4 18.1 %project.1 = (bf16[2,768,512]{2,1,0:T(8,128)(2,1)}, bf16[4,768,128]{2,1,0:T(8,128)(2,1)}, bf16[2,768,512]{2,1,0:T(8,128)(2,1)}, bf16[32,16,1024]{2,1,0:T(8,128)(...) custom-call(s32[5,64]{1,0:T(8,128)} %pad_add_fusion.refs_0_, ...), custom_call_target="tpu_custom_call" | custom-call | flops 8053063680 | bytes 20971520 | tf_op jit(solution)/shard_map/project/pallas_call | solution.py:232
  101.9 24.8 %back.1 = (bf16[64,16,2048]{2,1,0:T(8,128)(2,1)}, bf16[32,32,512]{2,1,0:T(8,128)(2,1)}, bf16[32,32,512]{2,1,0:T(8,128)(2,1)}, bf16[32,32,512]{2,1,0:T(8,128)(2,1...) custom-call(s32[5,64]{1,0:T(8,128)} %pad_add_fusion.refs_0_, ...), custom_call_target="tpu_custom_call" | custom-call | flops 8053063680 | bytes 20971520 | tf_op jit(solution)/shard_map/back/pallas_call | solution.py:333
  128.7 1.5 copy-done.31
  130.2 1.9 fusion.5
  132.1 3.9 %collective-permute-start.29 = (f32[384,2048]{1,0:T(8,128)S(1)}, f32[384,2048]{1,0:T(8,128)S(1)}, u32[]{:S(2)}, u32[]{:S(2)}) collective-permute-start(f32[384,2048]{1,0:T(8,128)S(1)} %fusion.5), channel_id=1, source_target_pairs={{0,1},{1,0},{2,3},{3,2},{4,5},{5,4},{6,7},{7,6},{8,9},{9,8},{10,11... | collective-permute-start | bytes 9437192 | tf_op jit(solution)/shard_map/ppermute | solution.py:71
  136.0 2.7 %collective-permute-start.26 = (bf16[32,32,512]{2,1,0:T(8,128)(2,1)S(1)}, bf16[32,32,512]{2,1,0:T(8,128)(2,1)S(1)}, u32[]{:S(2)}, u32[]{:S(2)}) collective-permute-start(bf16[32,32,512]{2,1,0:T(8,128)(2,1)S(1)} %copy-done.28), channel_id=1, source_target_pairs={{0,8},{1,25},{2,10},{3,27},{4,12},{5,29},{6,14},{7,31},{8,0},{9,17... | collective-permute-start | bytes 3145736 | tf_op jit(solution)/shard_map/ppermute | solution.py:63
  139.1 1.5 collective-permute-start.33
  140.6 2.3 %collective-permute-start.28 = (bf16[16,16,1024]{2,1,0:T(8,128)(2,1)S(1)}, bf16[16,16,1024]{2,1,0:T(8,128)(2,1)S(1)}, u32[]{:S(2)}, u32[]{:S(2)}) collective-permute-start(bf16[16,16,1024]{2,1,0:T(8,128)(2,1)S(1)} %get-tuple-element.102), channel_id=1, source_target_pairs={{0,2},{1,7},{2,0},{3,5},{4,6},{5,3},{6,4},{7,1},{8,10},{9,15},{10,... | collective-permute-start | bytes 1572872 | tf_op jit(solution)/shard_map/ppermute | solution.py:63
  142.9 8.0 %collective-permute-done.26 = bf16[32,32,512]{2,1,0:T(8,128)(2,1)S(1)} collective-permute-done((bf16[32,32,512]{2,1,0:T(8,128)(2,1)S(1)}, bf16[32,32,512]{2,1,0:T(8,128)(2,1)S(1)}, u32[]{:S(2)}, u32[]{:S(2)}) %collective-permute-start.26) | collective-permute-done | bytes 1048608 | tf_op jit(solution)/shard_map/ppermute | solution.py:63
  150.9 2.7 %collective-permute-start.27 = (bf16[16,16,1024]{2,1,0:T(8,128)(2,1)S(1)}, bf16[16,16,1024]{2,1,0:T(8,128)(2,1)S(1)}, u32[]{:S(2)}, u32[]{:S(2)}) collective-permute-start(bf16[16,16,1024]{2,1,0:T(8,128)(2,1)S(1)} %get-tuple-element.104), channel_id=1, source_target_pairs={{0,8},{1,25},{2,10},{3,27},{4,12},{5,29},{6,14},{7,31},{8,0},{9,17... | collective-permute-start | bytes 1572872 | tf_op jit(solution)/shard_map/ppermute | solution.py:63
  154.1 1.6 collective-permute-start.36
  156.6 3.5 %collective-permute-done.27 = bf16[16,16,1024]{2,1,0:T(8,128)(2,1)S(1)} collective-permute-done((bf16[16,16,1024]{2,1,0:T(8,128)(2,1)S(1)}, bf16[16,16,1024]{2,1,0:T(8,128)(2,1)S(1)}, u32[]{:S(2)}, u32[]{:S(2)}) %collective-permute-start.27) | collective-permute-done | bytes 524320 | tf_op jit(solution)/shard_map/ppermute | solution.py:63
  160.1 2.4 %collective-permute-start.34 = (bf16[16,32,512]{2,1,0:T(8,128)(2,1)S(1)}, bf16[16,32,512]{2,1,0:T(8,128)(2,1)S(1)}, u32[]{:S(2)}, u32[]{:S(2)}) collective-permute-start(bf16[16,32,512]{2,1,0:T(8,128)(2,1)S(1)} %get-tuple-element.98), channel_id=1, source_target_pairs={{0,2},{1,7},{2,0},{3,5},{4,6},{5,3},{6,4},{7,1},{8,10},{9,15},{10,... | collective-permute-start | bytes 1572872 | tf_op jit(solution)/shard_map/ppermute | solution.py:63
  162.7 1.6 collective-permute-start.38
  165.5 3.0 %add_convert_fusion = bf16[384,2048]{1,0:T(8,128)(2,1)} fusion(f32[384,2048]{1,0:T(8,128)S(1)} %collective-permute-done.29, bf16[384,1024]{1,0:T(8,128)(2,1)S(1)} %fusion.4, bf16[1024,2048]{1,0:T(8,128)(2,1)S(1)} %bitcast.92), kind=kOutput, calls=%fused_computation.8 | convolution fusion | flops 1612185600 | bytes 9699328 | tf_op jit(solution)/shard_map/dot_general | solution.py:500
  168.5 2.4 %collective-permute-start.37 = (bf16[8,32,512]{2,1,0:T(8,128)(2,1)S(1)}, bf16[8,32,512]{2,1,0:T(8,128)(2,1)S(1)}, u32[]{:S(2)}, u32[]{:S(2)}) collective-permute-start(bf16[8,32,512]{2,1,0:T(8,128)(2,1)S(1)} %add_convert_fusion.16), channel_id=1, source_target_pairs={{0,2},{1,7},{2,0},{3,5},{4,6},{5,3},{6,4},{7,1},{8,10},{9,15},{10,... | collective-permute-start | bytes 786440 | tf_op jit(solution)/shard_map/ppermute | solution.py:63
  172.3 1.6 collective-permute-start.32
  174.0 4.8 %collective-permute-done.32 = bf16[8,32,512]{2,1,0:T(8,128)(2,1)S(1)} collective-permute-done((bf16[8,32,512]{2,1,0:T(8,128)(2,1)S(1)}, bf16[8,32,512]{2,1,0:T(8,128)(2,1)S(1)}, u32[]{:S(2)}, u32[]{:S(2)}) %collective-permute-start.32) | collective-permute-done | bytes 262176 | tf_op jit(solution)/shard_map/ppermute | solution.py:63
  179.5 2.5 %collective-permute-start.41 = (bf16[2,160,512]{2,1,0:T(8,128)(2,1)S(1)}, bf16[2,160,512]{2,1,0:T(8,128)(2,1)S(1)}, u32[]{:S(2)}, u32[]{:S(2)}) collective-permute-start(bf16[2,160,512]{2,1,0:T(8,128)(2,1)S(1)} %get-tuple-element.109), channel_id=1, source_target_pairs={{0,24},{1,9},{2,26},{3,11},{4,28},{5,13},{6,30},{7,15},{8,16},{9,1... | collective-permute-start | bytes 983048 | tf_op jit(solution)/shard_map/ppermute | solution.py:63
  182.1 4.5 %collective-permute-done.40 = bf16[2,160,512]{2,1,0:T(8,128)(2,1)S(1)} collective-permute-done((bf16[2,160,512]{2,1,0:T(8,128)(2,1)S(1)}, bf16[2,160,512]{2,1,0:T(8,128)(2,1)S(1)}, u32[]{:S(2)}, u32[]{:S(2)}) %collective-permute-start.40) | collective-permute-done | bytes 327712 | tf_op jit(solution)/shard_map/ppermute | solution.py:63
  186.6 2.7 %collective-permute-done.42 = bf16[2,160,512]{2,1,0:T(8,128)(2,1)S(1)} collective-permute-done((bf16[2,160,512]{2,1,0:T(8,128)(2,1)S(1)}, bf16[2,160,512]{2,1,0:T(8,128)(2,1)S(1)}, u32[]{:S(2)}, u32[]{:S(2)}) %collective-permute-start.42) | collective-permute-done | bytes 327712 | tf_op jit(solution)/shard_map/ppermute | solution.py:63
  189.6 4.2 %collective-permute-done.43 = bf16[160,512]{1,0:T(8,128)(2,1)S(1)} collective-permute-done((bf16[160,512]{1,0:T(8,128)(2,1)S(1)}, bf16[160,512]{1,0:T(8,128)(2,1)S(1)}, u32[]{:S(2)}, u32[]{:S(2)}) %collective-permute-start.43) | collective-permute-done | bytes 163872 | tf_op jit(solution)/shard_map/ppermute | solution.py:63
  194.6 9.3 %all-to-all-start = ((f32[128,1,128]{2,1,0:T(1,128)}), f32[128,1,128]{2,1,0:T(1,128)S(1)}, u32[]{:S(2)}, u32[]{:S(2)}) async-start(f32[128,1,128]{2,1,0:T(1,128)} %broadcast_in_dim.2), calls=%async_computation | async-start | bytes 131072 | tf_op jit(solution)/shard_map/all_to_all | solution.py:515
  205.0 4.1 %collective-permute-start.45 = (f32[16,2048]{1,0:T(8,128)S(1)}, f32[16,2048]{1,0:T(8,128)S(1)}, u32[]{:S(2)}, u32[]{:S(2)}) collective-permute-start(f32[16,2048]{1,0:T(8,128)S(1)} %pad_maximum_fusion.8), channel_id=1, source_target_pairs={{0,0},{32,1},{2,2},{34,3},{4,4},{36,5},{6,6},{38,7},{8,8},{40,9},{... | collective-permute-start | bytes 393224 | tf_op jit(solution)/shard_map/ppermute | solution.py:530
  209.1 4.0 %all-to-all-done = f32[128,1,128]{2,1,0:T(1,128)S(1)} async-done(((f32[128,1,128]{2,1,0:T(1,128)}), f32[128,1,128]{2,1,0:T(1,128)S(1)}, u32[]{:S(2)}, u32[]{:S(2)}) %all-to-all-start) | async-done | bytes 65568 | tf_op jit(solution)/shard_map/all_to_all | solution.py:515
  (208 shorter events, 33.7 us)
Async XLA Ops:
  1.7 9.0 %collective-permute-start.2 = (bf16[16,2048]{1,0:T(8,128)(2,1)S(1)}, bf16[16,2048]{1,0:T(8,128)(2,1)S(1)}, u32[]{:S(2)}, u32[]{:S(2)}) collective-permute-start(bf16[16,2048]{1,0:T(8,128)(2,1)S(1)} %convert_element_type.270), channel_id=1, source_target_pairs={{0,0},{1,32},{2,2},{3,34},{4,4},{5,36},{6,6},{7,38},{8,8},{9,40},{... | collective-permute-start | bytes 196616 | tf_op jit(solution)/shard_map/ppermute | solution.py:453
  7.2 3.4 %collective-permute-start = (bf16[16,1536]{1,0:T(8,128)(2,1)S(1)}, bf16[16,1536]{1,0:T(8,128)(2,1)S(1)}, u32[]{:S(2)}, u32[]{:S(2)}) collective-permute-start(bf16[16,1536]{1,0:T(8,128)(2,1)S(1)} %broadcast_select_fusion.3), channel_id=1, source_target_pairs={{0,1},{1,0},{2,3},{3,2},{4,5},{5,4},{6,7},{7,6},{8,9},{9,8},{10,11... | collective-permute-start | bytes 147464 | tf_op jit(solution)/shard_map/ppermute | solution.py:71
  10.7 4.6 %collective-permute-start.3 = (bf16[160,512]{1,0:T(8,128)(2,1)S(1)}, bf16[160,512]{1,0:T(8,128)(2,1)S(1)}, u32[]{:S(2)}, u32[]{:S(2)}) collective-permute-start(bf16[160,512]{1,0:T(8,128)(2,1)S(1)} %constant_dynamic-update-slice_fusion), channel_id=1, source_target_pairs={{0,96},{1,33},{2,98},{3,35},{4,100},{5,37},{6,102},{7,39},{8,104},... | collective-permute-start | bytes 491528 | tf_op jit(solution)/shard_map/ppermute | solution.py:63
  15.4 12.5 %collective-permute-start.6 = (bf16[2,160,512]{2,1,0:T(8,128)(2,1)S(1)}, bf16[2,160,512]{2,1,0:T(8,128)(2,1)}, u32[]{:S(2)}, u32[]{:S(2)}) collective-permute-start(bf16[2,160,512]{2,1,0:T(8,128)(2,1)S(1)} %pad_maximum_fusion.7.refs_0_), channel_id=1, source_target_pairs={{0,30},{1,11},{2,28},{3,9},{4,26},{5,15},{6,24},{7,13},{8,22},{9,3... | collective-permute-start | bytes 983048 | tf_op jit(solution)/shard_map/ppermute | solution.py:63
  18.2 9.8 %collective-permute-start.5 = (bf16[2,160,512]{2,1,0:T(8,128)(2,1)S(1)}, bf16[2,160,512]{2,1,0:T(8,128)(2,1)}, u32[]{:S(2)}, u32[]{:S(2)}) collective-permute-start(bf16[2,160,512]{2,1,0:T(8,128)(2,1)S(1)} %pad_maximum_fusion.7.refs_0_), channel_id=1, source_target_pairs={{0,6},{1,3},{2,4},{3,1},{4,2},{5,7},{6,0},{7,5},{8,14},{9,11},{10,... | collective-permute-start | bytes 983048 | tf_op jit(solution)/shard_map/ppermute | solution.py:63
  18.2 9.8 %collective-permute-start.4 = (bf16[2,160,512]{2,1,0:T(8,128)(2,1)S(1)}, bf16[2,160,512]{2,1,0:T(8,128)(2,1)}, u32[]{:S(2)}, u32[]{:S(2)}) collective-permute-start(bf16[2,160,512]{2,1,0:T(8,128)(2,1)S(1)} %pad_maximum_fusion.7.refs_0_), channel_id=1, source_target_pairs={{0,24},{1,9},{2,26},{3,11},{4,28},{5,13},{6,30},{7,15},{8,16},{9,1... | collective-permute-start | bytes 983048 | tf_op jit(solution)/shard_map/ppermute | solution.py:63
  18.5 7.5 %collective-permute-start.21 = (s32[384]{0:T(512)S(1)}, s32[384]{0:T(512)S(1)}, u32[]{:S(2)}, u32[]{:S(2)}) collective-permute-start(s32[384]{0:T(512)S(1)} %copy-done.24), channel_id=1, source_target_pairs={{0,1},{1,0},{2,3},{3,2},{4,5},{5,4},{6,7},{7,6},{8,9},{9,8},{10,11... | collective-permute-start | bytes 4616 | tf_op jit(solution)/shard_map/ppermute | solution.py:71
  25.8 41.7 %collective-permute-start.1 = (bf16[384,2048]{1,0:T(8,128)(2,1)S(1)}, bf16[384,2048]{1,0:T(8,128)(2,1)S(1)}, u32[]{:S(2)}, u32[]{:S(2)}) collective-permute-start(bf16[384,2048]{1,0:T(8,128)(2,1)S(1)} %copy-done), channel_id=1, source_target_pairs={{0,1},{1,0},{2,3},{3,2},{4,5},{5,4},{6,7},{7,6},{8,9},{9,8},{10,11... | collective-permute-start | bytes 4718600 | tf_op jit(solution)/shard_map/ppermute | solution.py:71
  26.0 43.0 %collective-permute-start.17 = (bf16[384,2048]{1,0:T(8,128)(2,1)}, bf16[384,2048]{1,0:T(8,128)(2,1)}, u32[]{:S(2)}, u32[]{:S(2)}) collective-permute-start(bf16[384,2048]{1,0:T(8,128)(2,1)} %refs_3_.3), channel_id=1, source_target_pairs={{0,1},{1,0},{2,3},{3,2},{4,5},{5,4},{6,7},{7,6},{8,9},{9,8},{10,11... | collective-permute-start | bytes 4718600 | tf_op jit(solution)/shard_map/ppermute | solution.py:71
  30.8 13.6 %collective-permute-start.7 = (bf16[8,32,512]{2,1,0:T(8,128)(2,1)}, bf16[8,32,512]{2,1,0:T(8,128)(2,1)S(1)}, u32[]{:S(2)}, u32[]{:S(2)}) collective-permute-start(bf16[8,32,512]{2,1,0:T(8,128)(2,1)} %get-tuple-element.48), channel_id=1, source_target_pairs={{0,32},{1,97},{2,34},{3,99},{4,36},{5,101},{6,38},{7,103},{8,40},{... | collective-permute-start | bytes 786440 | tf_op jit(solution)/shard_map/ppermute | solution.py:63
  32.3 13.3 %collective-permute-start.11 = (bf16[8,32,512]{2,1,0:T(8,128)(2,1)}, bf16[8,32,512]{2,1,0:T(8,128)(2,1)S(1)}, u32[]{:S(2)}, u32[]{:S(2)}) collective-permute-start(bf16[8,32,512]{2,1,0:T(8,128)(2,1)} %get-tuple-element.50), channel_id=1, source_target_pairs={{0,2},{1,7},{2,0},{3,5},{4,6},{5,3},{6,4},{7,1},{8,10},{9,15},{10,... | collective-permute-start | bytes 786440 | tf_op jit(solution)/shard_map/ppermute | solution.py:63
  34.9 6.7 %collective-permute-start.15 = (bf16[8,16,1024]{2,1,0:T(8,128)(2,1)}, bf16[8,16,1024]{2,1,0:T(8,128)(2,1)S(1)}, u32[]{:S(2)}, u32[]{:S(2)}) collective-permute-start(bf16[8,16,1024]{2,1,0:T(8,128)(2,1)} %get-tuple-element.52), channel_id=1, source_target_pairs={{0,8},{1,25},{2,10},{3,27},{4,12},{5,29},{6,14},{7,31},{8,0},{9,17... | collective-permute-start | bytes 786440 | tf_op jit(solution)/shard_map/ppermute | solution.py:63
  41.6 6.4 %collective-permute-start.9 = (bf16[8,32,512]{2,1,0:T(8,128)(2,1)S(1)}, bf16[8,32,512]{2,1,0:T(8,128)(2,1)S(1)}, u32[]{:S(2)}, u32[]{:S(2)}) collective-permute-start(bf16[8,32,512]{2,1,0:T(8,128)(2,1)S(1)} %copy-done.10), channel_id=1, source_target_pairs={{0,8},{1,25},{2,10},{3,27},{4,12},{5,29},{6,14},{7,31},{8,0},{9,17... | collective-permute-start | bytes 786440 | tf_op jit(solution)/shard_map/ppermute | solution.py:63
  44.3 6.5 %collective-permute-start.13 = (bf16[8,16,1024]{2,1,0:T(8,128)(2,1)S(1)}, bf16[8,16,1024]{2,1,0:T(8,128)(2,1)S(1)}, u32[]{:S(2)}, u32[]{:S(2)}) collective-permute-start(bf16[8,16,1024]{2,1,0:T(8,128)(2,1)S(1)} %copy-done.9), channel_id=1, source_target_pairs={{0,32},{1,97},{2,34},{3,99},{4,36},{5,101},{6,38},{7,103},{8,40},{... | collective-permute-start | bytes 786440 | tf_op jit(solution)/shard_map/ppermute | solution.py:63
  45.6 9.3 %collective-permute-start.8 = (bf16[16,32,512]{2,1,0:T(8,128)(2,1)S(1)}, bf16[16,32,512]{2,1,0:T(8,128)(2,1)S(1)}, u32[]{:S(2)}, u32[]{:S(2)}) collective-permute-start(bf16[16,32,512]{2,1,0:T(8,128)(2,1)S(1)} %pad_maximum_fusion.2), channel_id=1, source_target_pairs={{0,8},{1,25},{2,10},{3,27},{4,12},{5,29},{6,14},{7,31},{8,0},{9,17... | collective-permute-start | bytes 1572872 | tf_op jit(solution)/shard_map/ppermute | solution.py:63
  48.0 9.2 %collective-permute-start.12 = (bf16[16,32,512]{2,1,0:T(8,128)(2,1)S(1)}, bf16[16,32,512]{2,1,0:T(8,128)(2,1)S(1)}, u32[]{:S(2)}, u32[]{:S(2)}) collective-permute-start(bf16[16,32,512]{2,1,0:T(8,128)(2,1)S(1)} %pad_maximum_fusion.4), channel_id=1, source_target_pairs={{0,32},{1,97},{2,34},{3,99},{4,36},{5,101},{6,38},{7,103},{8,40},{... | collective-permute-start | bytes 1572872 | tf_op jit(solution)/shard_map/ppermute | solution.py:63
  50.8 9.2 %collective-permute-start.10 = (bf16[16,32,512]{2,1,0:T(8,128)(2,1)S(1)}, bf16[16,32,512]{2,1,0:T(8,128)(2,1)S(1)}, u32[]{:S(2)}, u32[]{:S(2)}) collective-permute-start(bf16[16,32,512]{2,1,0:T(8,128)(2,1)S(1)} %pad_maximum_fusion.3), channel_id=1, source_target_pairs={{0,2},{1,7},{2,0},{3,5},{4,6},{5,3},{6,4},{7,1},{8,10},{9,15},{10,... | collective-permute-start | bytes 1572872 | tf_op jit(solution)/shard_map/ppermute | solution.py:63
  55.0 9.2 %collective-permute-start.14 = (bf16[16,16,1024]{2,1,0:T(8,128)(2,1)S(1)}, bf16[16,16,1024]{2,1,0:T(8,128)(2,1)S(1)}, u32[]{:S(2)}, u32[]{:S(2)}) collective-permute-start(bf16[16,16,1024]{2,1,0:T(8,128)(2,1)S(1)} %pad_maximum_fusion.5), channel_id=1, source_target_pairs={{0,8},{1,25},{2,10},{3,27},{4,12},{5,29},{6,14},{7,31},{8,0},{9,17... | collective-permute-start | bytes 1572872 | tf_op jit(solution)/shard_map/ppermute | solution.py:63
  57.3 9.3 %collective-permute-start.16 = (bf16[16,16,1024]{2,1,0:T(8,128)(2,1)S(1)}, bf16[16,16,1024]{2,1,0:T(8,128)(2,1)S(1)}, u32[]{:S(2)}, u32[]{:S(2)}) collective-permute-start(bf16[16,16,1024]{2,1,0:T(8,128)(2,1)S(1)} %pad_maximum_fusion.6), channel_id=1, source_target_pairs={{0,2},{1,7},{2,0},{3,5},{4,6},{5,3},{6,4},{7,1},{8,10},{9,15},{10,... | collective-permute-start | bytes 1572872 | tf_op jit(solution)/shard_map/ppermute | solution.py:63
  60.1 15.4 %collective-permute-start.20 = (bf16[32,32,512]{2,1,0:T(8,128)(2,1)S(1)}, bf16[32,32,512]{2,1,0:T(8,128)(2,1)S(1)}, u32[]{:S(2)}, u32[]{:S(2)}) collective-permute-start(bf16[32,32,512]{2,1,0:T(8,128)(2,1)S(1)} %constant_dynamic-update-slice_fusion.16.refs_9_), channel_id=1, source_target_pairs={{0,8},{1,25},{2,10},{3,27},{4,12},{5,29},{6,14},{7,31},{8,0},{9,17... | collective-permute-start | bytes 3145736 | tf_op jit(solution)/shard_map/ppermute | solution.py:63
  64.2 14.9 %collective-permute-start.19 = (bf16[32,32,512]{2,1,0:T(8,128)(2,1)S(1)}, bf16[32,32,512]{2,1,0:T(8,128)(2,1)S(1)}, u32[]{:S(2)}, u32[]{:S(2)}) collective-permute-start(bf16[32,32,512]{2,1,0:T(8,128)(2,1)S(1)} %constant_dynamic-update-slice_fusion.13.refs_7_), channel_id=1, source_target_pairs={{0,32},{1,97},{2,34},{3,99},{4,36},{5,101},{6,38},{7,103},{8,40},{... | collective-permute-start | bytes 3145736 | tf_op jit(solution)/shard_map/ppermute | solution.py:63
  66.6 14.9 %collective-permute-start.18 = (bf16[32,32,512]{2,1,0:T(8,128)(2,1)S(1)}, bf16[32,32,512]{2,1,0:T(8,128)(2,1)S(1)}, u32[]{:S(2)}, u32[]{:S(2)}) collective-permute-start(bf16[32,32,512]{2,1,0:T(8,128)(2,1)S(1)} %constant_dynamic-update-slice_fusion.10.refs_5_), channel_id=1, source_target_pairs={{0,2},{1,7},{2,0},{3,5},{4,6},{5,3},{6,4},{7,1},{8,10},{9,15},{10,... | collective-permute-start | bytes 3145736 | tf_op jit(solution)/shard_map/ppermute | solution.py:63
  67.5 34.4 %collective-permute-start.23 = (bf16[32,16,1024]{2,1,0:T(8,128)(2,1)}, bf16[32,16,1024]{2,1,0:T(8,128)(2,1)}, u32[]{:S(2)}, u32[]{:S(2)}) collective-permute-start(bf16[32,16,1024]{2,1,0:T(8,128)(2,1)} %constant_dynamic-update-slice_fusion.22.refs_7_), channel_id=1, source_target_pairs={{0,32},{1,97},{2,34},{3,99},{4,36},{5,101},{6,38},{7,103},{8,40},{... | collective-permute-start | bytes 3145736 | tf_op jit(solution)/shard_map/ppermute | solution.py:63
  69.1 32.8 %collective-permute-start.22 = (bf16[32,16,1024]{2,1,0:T(8,128)(2,1)}, bf16[32,16,1024]{2,1,0:T(8,128)(2,1)}, u32[]{:S(2)}, u32[]{:S(2)}) collective-permute-start(bf16[32,16,1024]{2,1,0:T(8,128)(2,1)} %constant_dynamic-update-slice_fusion.19.refs_5_), channel_id=1, source_target_pairs={{0,2},{1,7},{2,0},{3,5},{4,6},{5,3},{6,4},{7,1},{8,10},{9,15},{10,... | collective-permute-start | bytes 3145736 | tf_op jit(solution)/shard_map/ppermute | solution.py:63
  100.6 26.1 %collective-permute-start.25 = (bf16[32,16,1024]{2,1,0:T(8,128)(2,1)}, bf16[32,16,1024]{2,1,0:T(8,128)(2,1)S(1)}, u32[]{:S(2)}, u32[]{:S(2)}) collective-permute-start(bf16[32,16,1024]{2,1,0:T(8,128)(2,1)} %get-tuple-element.68), channel_id=1, source_target_pairs={{0,32},{1,97},{2,34},{3,99},{4,36},{5,101},{6,38},{7,103},{8,40},{... | collective-permute-start | bytes 3145736 | tf_op jit(solution)/shard_map/ppermute | solution.py:63
  101.8 25.3 %collective-permute-start.24 = (bf16[32,16,1024]{2,1,0:T(8,128)(2,1)}, bf16[32,16,1024]{2,1,0:T(8,128)(2,1)S(1)}, u32[]{:S(2)}, u32[]{:S(2)}) collective-permute-start(bf16[32,16,1024]{2,1,0:T(8,128)(2,1)} %get-tuple-element.58), channel_id=1, source_target_pairs={{0,2},{1,7},{2,0},{3,5},{4,6},{5,3},{6,4},{7,1},{8,10},{9,15},{10,... | collective-permute-start | bytes 3145736 | tf_op jit(solution)/shard_map/ppermute | solution.py:63
  132.1 32.4 %collective-permute-start.29 = (f32[384,2048]{1,0:T(8,128)S(1)}, f32[384,2048]{1,0:T(8,128)S(1)}, u32[]{:S(2)}, u32[]{:S(2)}) collective-permute-start(f32[384,2048]{1,0:T(8,128)S(1)} %fusion.5), channel_id=1, source_target_pairs={{0,1},{1,0},{2,3},{3,2},{4,5},{5,4},{6,7},{7,6},{8,9},{9,8},{10,11... | collective-permute-start | bytes 9437192 | tf_op jit(solution)/shard_map/ppermute | solution.py:71
  136.0 14.9 %collective-permute-start.26 = (bf16[32,32,512]{2,1,0:T(8,128)(2,1)S(1)}, bf16[32,32,512]{2,1,0:T(8,128)(2,1)S(1)}, u32[]{:S(2)}, u32[]{:S(2)}) collective-permute-start(bf16[32,32,512]{2,1,0:T(8,128)(2,1)S(1)} %copy-done.28), channel_id=1, source_target_pairs={{0,8},{1,25},{2,10},{3,27},{4,12},{5,29},{6,14},{7,31},{8,0},{9,17... | collective-permute-start | bytes 3145736 | tf_op jit(solution)/shard_map/ppermute | solution.py:63
  138.7 15.4 %collective-permute-start.30 = (bf16[32,32,512]{2,1,0:T(8,128)(2,1)S(1)}, bf16[32,32,512]{2,1,0:T(8,128)(2,1)S(1)}, u32[]{:S(2)}, u32[]{:S(2)}) collective-permute-start(bf16[32,32,512]{2,1,0:T(8,128)(2,1)S(1)} %copy-done.26), channel_id=1, source_target_pairs={{0,2},{1,7},{2,0},{3,5},{4,6},{5,3},{6,4},{7,1},{8,10},{9,15},{10,... | collective-permute-start | bytes 3145736 | tf_op jit(solution)/shard_map/ppermute | solution.py:63
  139.1 17.0 %collective-permute-start.33 = (bf16[32,32,512]{2,1,0:T(8,128)(2,1)S(1)}, bf16[32,32,512]{2,1,0:T(8,128)(2,1)S(1)}, u32[]{:S(2)}, u32[]{:S(2)}) collective-permute-start(bf16[32,32,512]{2,1,0:T(8,128)(2,1)S(1)} %copy-done.25), channel_id=1, source_target_pairs={{0,32},{1,97},{2,34},{3,99},{4,36},{5,101},{6,38},{7,103},{8,40},{... | collective-permute-start | bytes 3145736 | tf_op jit(solution)/shard_map/ppermute | solution.py:63
  140.6 22.1 %collective-permute-start.28 = (bf16[16,16,1024]{2,1,0:T(8,128)(2,1)S(1)}, bf16[16,16,1024]{2,1,0:T(8,128)(2,1)S(1)}, u32[]{:S(2)}, u32[]{:S(2)}) collective-permute-start(bf16[16,16,1024]{2,1,0:T(8,128)(2,1)S(1)} %get-tuple-element.102), channel_id=1, source_target_pairs={{0,2},{1,7},{2,0},{3,5},{4,6},{5,3},{6,4},{7,1},{8,10},{9,15},{10,... | collective-permute-start | bytes 1572872 | tf_op jit(solution)/shard_map/ppermute | solution.py:63
  150.9 9.2 %collective-permute-start.27 = (bf16[16,16,1024]{2,1,0:T(8,128)(2,1)S(1)}, bf16[16,16,1024]{2,1,0:T(8,128)(2,1)S(1)}, u32[]{:S(2)}, u32[]{:S(2)}) collective-permute-start(bf16[16,16,1024]{2,1,0:T(8,128)(2,1)S(1)} %get-tuple-element.104), channel_id=1, source_target_pairs={{0,8},{1,25},{2,10},{3,27},{4,12},{5,29},{6,14},{7,31},{8,0},{9,17... | collective-permute-start | bytes 1572872 | tf_op jit(solution)/shard_map/ppermute | solution.py:63
  154.1 14.3 %collective-permute-start.36 = (bf16[16,32,512]{2,1,0:T(8,128)(2,1)S(1)}, bf16[16,32,512]{2,1,0:T(8,128)(2,1)S(1)}, u32[]{:S(2)}, u32[]{:S(2)}) collective-permute-start(bf16[16,32,512]{2,1,0:T(8,128)(2,1)S(1)} %get-tuple-element.96), channel_id=1, source_target_pairs={{0,32},{1,97},{2,34},{3,99},{4,36},{5,101},{6,38},{7,103},{8,40},{... | collective-permute-start | bytes 1572872 | tf_op jit(solution)/shard_map/ppermute | solution.py:63
  156.1 16.1 %collective-permute-start.31 = (bf16[16,32,512]{2,1,0:T(8,128)(2,1)S(1)}, bf16[16,32,512]{2,1,0:T(8,128)(2,1)S(1)}, u32[]{:S(2)}, u32[]{:S(2)}) collective-permute-start(bf16[16,32,512]{2,1,0:T(8,128)(2,1)S(1)} %get-tuple-element.100), channel_id=1, source_target_pairs={{0,8},{1,25},{2,10},{3,27},{4,12},{5,29},{6,14},{7,31},{8,0},{9,17... | collective-permute-start | bytes 1572872 | tf_op jit(solution)/shard_map/ppermute | solution.py:63
  160.1 10.8 %collective-permute-start.34 = (bf16[16,32,512]{2,1,0:T(8,128)(2,1)S(1)}, bf16[16,32,512]{2,1,0:T(8,128)(2,1)S(1)}, u32[]{:S(2)}, u32[]{:S(2)}) collective-permute-start(bf16[16,32,512]{2,1,0:T(8,128)(2,1)S(1)} %get-tuple-element.98), channel_id=1, source_target_pairs={{0,2},{1,7},{2,0},{3,5},{4,6},{5,3},{6,4},{7,1},{8,10},{9,15},{10,... | collective-permute-start | bytes 1572872 | tf_op jit(solution)/shard_map/ppermute | solution.py:63
  162.7 11.3 %collective-permute-start.38 = (bf16[8,16,1024]{2,1,0:T(8,128)(2,1)S(1)}, bf16[8,16,1024]{2,1,0:T(8,128)(2,1)S(1)}, u32[]{:S(2)}, u32[]{:S(2)}) collective-permute-start(bf16[8,16,1024]{2,1,0:T(8,128)(2,1)S(1)} %get-tuple-element.113), channel_id=1, source_target_pairs={{0,32},{1,97},{2,34},{3,99},{4,36},{5,101},{6,38},{7,103},{8,40},{... | collective-permute-start | bytes 786440 | tf_op jit(solution)/shard_map/ppermute | solution.py:63
  164.5 9.4 %collective-permute-start.39 = (bf16[8,16,1024]{2,1,0:T(8,128)(2,1)S(1)}, bf16[8,16,1024]{2,1,0:T(8,128)(2,1)S(1)}, u32[]{:S(2)}, u32[]{:S(2)}) collective-permute-start(bf16[8,16,1024]{2,1,0:T(8,128)(2,1)S(1)} %get-tuple-element.111), channel_id=1, source_target_pairs={{0,8},{1,25},{2,10},{3,27},{4,12},{5,29},{6,14},{7,31},{8,0},{9,17... | collective-permute-start | bytes 786440 | tf_op jit(solution)/shard_map/ppermute | solution.py:63
  168.5 10.5 %collective-permute-start.37 = (bf16[8,32,512]{2,1,0:T(8,128)(2,1)S(1)}, bf16[8,32,512]{2,1,0:T(8,128)(2,1)S(1)}, u32[]{:S(2)}, u32[]{:S(2)}) collective-permute-start(bf16[8,32,512]{2,1,0:T(8,128)(2,1)S(1)} %add_convert_fusion.16), channel_id=1, source_target_pairs={{0,2},{1,7},{2,0},{3,5},{4,6},{5,3},{6,4},{7,1},{8,10},{9,15},{10,... | collective-permute-start | bytes 786440 | tf_op jit(solution)/shard_map/ppermute | solution.py:63
  171.0 7.9 %collective-permute-start.35 = (bf16[8,32,512]{2,1,0:T(8,128)(2,1)S(1)}, bf16[8,32,512]{2,1,0:T(8,128)(2,1)S(1)}, u32[]{:S(2)}, u32[]{:S(2)}) collective-permute-start(bf16[8,32,512]{2,1,0:T(8,128)(2,1)S(1)} %add_convert_fusion.19), channel_id=1, source_target_pairs={{0,8},{1,25},{2,10},{3,27},{4,12},{5,29},{6,14},{7,31},{8,0},{9,17... | collective-permute-start | bytes 786440 | tf_op jit(solution)/shard_map/ppermute | solution.py:63
  172.3 6.5 %collective-permute-start.32 = (bf16[8,32,512]{2,1,0:T(8,128)(2,1)S(1)}, bf16[8,32,512]{2,1,0:T(8,128)(2,1)S(1)}, u32[]{:S(2)}, u32[]{:S(2)}) collective-permute-start(bf16[8,32,512]{2,1,0:T(8,128)(2,1)S(1)} %add_convert_fusion.22), channel_id=1, source_target_pairs={{0,32},{1,97},{2,34},{3,99},{4,36},{5,101},{6,38},{7,103},{8,40},{... | collective-permute-start | bytes 786440 | tf_op jit(solution)/shard_map/ppermute | solution.py:63
  179.3 7.2 %collective-permute-start.40 = (bf16[2,160,512]{2,1,0:T(8,128)(2,1)S(1)}, bf16[2,160,512]{2,1,0:T(8,128)(2,1)S(1)}, u32[]{:S(2)}, u32[]{:S(2)}) collective-permute-start(bf16[2,160,512]{2,1,0:T(8,128)(2,1)S(1)} %get-tuple-element.107), channel_id=1, source_target_pairs={{0,30},{1,11},{2,28},{3,9},{4,26},{5,15},{6,24},{7,13},{8,22},{9,3... | collective-permute-start | bytes 983048 | tf_op jit(solution)/shard_map/ppermute | solution.py:63
  179.4 9.8 %collective-permute-start.42 = (bf16[2,160,512]{2,1,0:T(8,128)(2,1)S(1)}, bf16[2,160,512]{2,1,0:T(8,128)(2,1)S(1)}, u32[]{:S(2)}, u32[]{:S(2)}) collective-permute-start(bf16[2,160,512]{2,1,0:T(8,128)(2,1)S(1)} %get-tuple-element.108), channel_id=1, source_target_pairs={{0,6},{1,3},{2,4},{3,1},{4,2},{5,7},{6,0},{7,5},{8,14},{9,11},{10,... | collective-permute-start | bytes 983048 | tf_op jit(solution)/shard_map/ppermute | solution.py:63
  179.5 9.7 %collective-permute-start.41 = (bf16[2,160,512]{2,1,0:T(8,128)(2,1)S(1)}, bf16[2,160,512]{2,1,0:T(8,128)(2,1)S(1)}, u32[]{:S(2)}, u32[]{:S(2)}) collective-permute-start(bf16[2,160,512]{2,1,0:T(8,128)(2,1)S(1)} %get-tuple-element.109), channel_id=1, source_target_pairs={{0,24},{1,9},{2,26},{3,11},{4,28},{5,13},{6,30},{7,15},{8,16},{9,1... | collective-permute-start | bytes 983048 | tf_op jit(solution)/shard_map/ppermute | solution.py:63
  189.5 25.2 %copy-start.13 = (f32[16,3072]{1,0:T(8,128)S(1)}, f32[16,3072]{1,0:T(8,128)}, u32[]{:S(2)}) copy-start(f32[16,3072]{1,0:T(8,128)} %param.14) | copy-start | bytes 589828
  189.5 4.2 %collective-permute-start.43 = (bf16[160,512]{1,0:T(8,128)(2,1)S(1)}, bf16[160,512]{1,0:T(8,128)(2,1)S(1)}, u32[]{:S(2)}, u32[]{:S(2)}) collective-permute-start(bf16[160,512]{1,0:T(8,128)(2,1)S(1)} %fusion.12), channel_id=1, source_target_pairs={{0,96},{1,33},{2,98},{3,35},{4,100},{5,37},{6,102},{7,39},{8,104},... | collective-permute-start | bytes 491528 | tf_op jit(solution)/shard_map/ppermute | solution.py:63
  194.6 18.6 %all-to-all-start = ((f32[128,1,128]{2,1,0:T(1,128)}), f32[128,1,128]{2,1,0:T(1,128)S(1)}, u32[]{:S(2)}, u32[]{:S(2)}) async-start(f32[128,1,128]{2,1,0:T(1,128)} %broadcast_in_dim.2), calls=%async_computation | async-start | bytes 131072 | tf_op jit(solution)/shard_map/all_to_all | solution.py:515
  203.9 10.6 %collective-permute-start.44 = (f32[3,16,512]{2,1,0:T(8,128)S(1)}, f32[3,16,512]{2,1,0:T(8,128)S(1)}, u32[]{:S(2)}, u32[]{:S(2)}) collective-permute-start(f32[3,16,512]{2,1,0:T(8,128)S(1)} %select_bitcast_fusion), channel_id=1, source_target_pairs={{0,1},{1,0},{2,3},{3,2},{4,5},{5,4},{6,7},{7,6},{8,9},{9,8},{10,11... | collective-permute-start | bytes 294920 | tf_op jit(solution)/shard_map/ppermute | solution.py:71
  205.0 10.5 %collective-permute-start.45 = (f32[16,2048]{1,0:T(8,128)S(1)}, f32[16,2048]{1,0:T(8,128)S(1)}, u32[]{:S(2)}, u32[]{:S(2)}) collective-permute-start(f32[16,2048]{1,0:T(8,128)S(1)} %pad_maximum_fusion.8), channel_id=1, source_target_pairs={{0,0},{32,1},{2,2},{34,3},{4,4},{36,5},{6,6},{38,7},{8,8},{40,9},{... | collective-permute-start | bytes 393224 | tf_op jit(solution)/shard_map/ppermute | solution.py:530
  (31 other events, 314.8 us)
where the time goes:
time: 217 us; the launch traced here: 216 us
  starting transfers between devices  80.7 us (37%)
  waiting for transfers between devices  56.2 us (26%)
  Pallas kernels  45.7 us (21%)
  other arithmetic  13.8 us (6%)
  local copies, waits for them, and re-layouts  12.8 us (6%)
  matrix products  4.85 us (2%)
  between operations  2.38 us (1%)
    ppermute x38, waiting for transfers between devices, across(): return lax.ppermute(x, ALL, pairs)  51.9 us
    ppermute x38, starting transfers between devices, across(): return lax.ppermute(x, ALL, pairs)  50.8 us
    pallas_call x1, Pallas kernels, backward(): pl.pallas_call(backward_body, in_specs=[SMEM] + [HBM] * 8 + [VMEM] * 4, o...  24.8 us
    pallas_call x1, Pallas kernels, project(): pl.pallas_call(project_body, in_specs=[SMEM] + [HBM] * 10 + [VMEM] * 2, o...  18.1 us
    ppermute x6, starting transfers between devices, to_partner(): return lax.ppermute(x, 'dp_2', [(0, 1), (1, 0)])  12.1 us
    unnamed x93, local copies, waits for them, and re-layouts  9.39 us
    all_to_all x1, starting transfers between devices, local(): lax.all_to_all(jnp.broadcast_to(squares, (128, 128)), ALL, split_axis=0,...  9.25 us
    ppermute x1, starting transfers between devices, local(): out_block = lax.ppermute(out_weight.astype(BF), ALL, out_pairs())  4.49 us
  transfers between devices with their start and end apart: 47, of which 19 were waited for; matrix products, arithmetic and copies ran while one was open for 10% of the time, Pallas kernels for 21%

commit v1 on v0

--- a/solution.py
+++ b/solution.py
@@ -369,22 +369,29 @@
     )(*ins)
 
 
-def by_stream(pieces):
+def qkv_streams(pieces):
     def pairs(*refs):
-        sources, outs = refs[:4], refs[4:]
-        copies = []
-        for i, src in enumerate(sources):
-            at = pl.ds(2 * i, 2)
-            for s in range(3):
-                copies.append((src.at[:, pl.ds(32 * s, 32)], outs[s].at[at]))
-            for j in range(4):
-                target = outs[3 + j // 2].at[at, :, pl.ds(512 * (j % 2), 512)]
-                copies.append((src.at[:, pl.ds(96 + 16 * j, 16)], target))
-        return copies
-
-    shapes = (jax.ShapeDtypeStruct((8, 32, 512), BF),) * 3
-    shapes += (jax.ShapeDtypeStruct((8, 16, 1024), BF),) * 2
-    return moved(pairs, pieces, shapes)
+        return [
+            (src.at[:, pl.ds(32 * s, 32)], refs[4 + s].at[pl.ds(2 * i, 2)])
+            for i, src in enumerate(refs[:4])
+            for s in range(3)
+        ]
+
+    return moved(pairs, pieces, (jax.ShapeDtypeStruct((8, 32, 512), BF),) * 3)
+
+
+def out_streams(pieces):
+    def pairs(*refs):
+        return [
+            (
+                src.at[:, pl.ds(96 + 16 * j, 16)],
+                refs[4 + j // 2].at[pl.ds(2 * i, 2), :, pl.ds(512 * (j % 2), 512)],
+            )
+            for i, src in enumerate(refs[:4])
+            for j in range(4)
+        ]
+
+    return moved(pairs, pieces, (jax.ShapeDtypeStruct((8, 16, 1024), BF),) * 2)
 
 
 def added(a, b):
@@ -458,7 +465,9 @@
         axis=0,
     )
     low = jnp.stack([block, early(block, 1)])
-    have = list(by_stream([low] + [early(low, p) for p in (2, 4, 6)]))
+    pieces = [low] + [early(low, p) for p in (2, 4, 6)]
+    have = list(qkv_streams(pieces))
+    have += out_streams(pieces)
 
     def gather(s, stage):
         return across(have[s], late_links(s % 3, stage))

time: 217 us -> 219 us (level)
  starting transfers between devices: 80.7 us -> 83.2 us
  waiting for transfers between devices: 56.2 us -> 54 us
    ppermute x38, starting transfers between devices: 50.8 us -> 55.3 us  [across(): return lax.ppermute(x, ALL, pairs)]
    ppermute x6, starting transfers between devices: 12.1 us -> 8.33 us  [to_partner(): return lax.ppermute(x, 'dp_2', [(0, 1), (1, 0)])]
    ppermute x38, waiting for transfers between devices: 51.9 us -> 49.7 us  [across(): return lax.ppermute(x, ALL, pairs)]
    pallas_call x1 -> x2, Pallas kernels: 2.75 us -> 4.57 us  [moved(): pl.pallas_call(kernel, in_specs=[HBM] * len(ins), out_specs=(VMEM,) * len...]
  transfers between devices with their start and end apart: 47 -> 47, of which waited for: 19 -> 19; matrix products, arithmetic and copies ran while one was open for 10% -> 10% of each run, Pallas kernels for 21% -> 22%
where the time goes in v1:
time: 219 us
  starting transfers between devices  83.2 us (38%)
  waiting for transfers between devices  54 us (25%)
  Pallas kernels  47.6 us (22%)
  other arithmetic  13.8 us (6%)
  local copies, waits for them, and re-layouts  12.8 us (6%)
  matrix products  4.85 us (2%)
  between operations  2.36 us (1%)
    ppermute x38, starting transfers between devices, across(): return lax.ppermute(x, ALL, pairs)  55.3 us
    ppermute x38, waiting for transfers between devices, across(): return lax.ppermute(x, ALL, pairs)  49.7 us
    pallas_call x1, Pallas kernels, backward(): pl.pallas_call(backward_body, in_specs=[SMEM] + [HBM] * 8 + [VMEM] * 4, o...  24.8 us
    pallas_call x1, Pallas kernels, project(): pl.pallas_call(project_body, in_specs=[SMEM] + [HBM] * 10 + [VMEM] * 2, o...  18.2 us
    all_to_all x1, starting transfers between devices, local(): lax.all_to_all(jnp.broadcast_to(squares, (128, 128)), ALL, split_axis=0,...  11 us
    unnamed x93, local copies, waits for them, and re-layouts  9.36 us
    ppermute x6, starting transfers between devices, to_partner(): return lax.ppermute(x, 'dp_2', [(0, 1), (1, 0)])  8.33 us
    pallas_call x2, Pallas kernels, moved(): pl.pallas_call(kernel, in_specs=[HBM] * len(ins), out_specs=(VMEM,) * len...  4.57 us
  transfers between devices with their start and end apart: 47, of which 19 were waited for; matrix products, arithmetic and copies ran while one was open for 10% of the time, Pallas kernels for 22%

profile of v1, /device:TPU:1, one launch (start us, length us, event | category | flops | bytes accessed | tf_op | source)
XLA Modules:
  0.0 218.7 jit_solution(5452584844250325322)
XLA Ops:
  1.7 4.5 %collective-permute-start.2 = (bf16[16,2048]{1,0:T(8,128)(2,1)S(1)}, bf16[16,2048]{1,0:T(8,128)(2,1)S(1)}, u32[]{:S(2)}, u32[]{:S(2)}) collective-permute-start(bf16[16,2048]{1,0:T(8,128)(2,1)S(1)} %convert_element_type.270), channel_id=1, source_target_pairs={{0,0},{1,32},{2,2},{3,34},{4,4},{5,36},{6,6},{7,38},{8,8},{9,40},{... | collective-permute-start | bytes 196616 | tf_op jit(solution)/shard_map/ppermute | solution.py:460
  7.3 1.8 fusion
  10.7 1.9 collective-permute-start.3
  12.7 2.7 %collective-permute-done.3 = bf16[160,512]{1,0:T(8,128)(2,1)S(1)} collective-permute-done((bf16[160,512]{1,0:T(8,128)(2,1)S(1)}, bf16[160,512]{1,0:T(8,128)(2,1)S(1)}, u32[]{:S(2)}, u32[]{:S(2)}) %collective-permute-start.3) | collective-permute-done | bytes 163872 | tf_op jit(solution)/shard_map/ppermute | solution.py:63
  15.4 2.7 %collective-permute-start.6 = (bf16[2,160,512]{2,1,0:T(8,128)(2,1)S(1)}, bf16[2,160,512]{2,1,0:T(8,128)(2,1)}, u32[]{:S(2)}, u32[]{:S(2)}) collective-permute-start(bf16[2,160,512]{2,1,0:T(8,128)(2,1)S(1)} %pad_maximum_fusion.7.refs_0_), channel_id=1, source_target_pairs={{0,30},{1,11},{2,28},{3,9},{4,26},{5,15},{6,24},{7,13},{8,22},{9,3... | collective-permute-start | bytes 983048 | tf_op jit(solution)/shard_map/ppermute | solution.py:63
  18.5 6.7 %collective-permute-start.21 = (s32[384]{0:T(512)S(1)}, s32[384]{0:T(512)S(1)}, u32[]{:S(2)}, u32[]{:S(2)}) collective-permute-start(s32[384]{0:T(512)S(1)} %copy-done.24), channel_id=1, source_target_pairs={{0,1},{1,0},{2,3},{3,2},{4,5},{5,4},{6,7},{7,6},{8,9},{9,8},{10,11... | collective-permute-start | bytes 4616 | tf_op jit(solution)/shard_map/ppermute | solution.py:71
  28.0 2.2 shard_map.163
  30.1 1.6 collective-permute-start.13
  31.7 2.4 %shard_map.162 = (bf16[8,32,512]{2,1,0:T(8,128)(2,1)}, bf16[8,32,512]{2,1,0:T(8,128)(2,1)}, bf16[8,32,512]{2,1,0:T(8,128)(2,1)}) custom-call(bf16[2,160,512]{2,1,0:T(8,128)(2,1)} %copy-done.1, bf16[2,160,512]{2,1,0:T(8,128)(2,1)} %collective-permute-done.4.refs_1_, bf16[2,160,512]{2,1,0:T(8,128)(2,1)} %collective-permute-done.5.refs_2_, ...), custom_call_target="tpu_custom_call" | custom-call | tf_op jit(solution)/shard_map/pallas_call | solution.py:363
  34.2 2.4 %collective-permute-start.9 = (bf16[8,32,512]{2,1,0:T(8,128)(2,1)}, bf16[8,32,512]{2,1,0:T(8,128)(2,1)S(1)}, u32[]{:S(2)}, u32[]{:S(2)}) collective-permute-start(bf16[8,32,512]{2,1,0:T(8,128)(2,1)} %get-tuple-element.49), channel_id=1, source_target_pairs={{0,8},{1,25},{2,10},{3,27},{4,12},{5,29},{6,14},{7,31},{8,0},{9,17... | collective-permute-start | bytes 786440 | tf_op jit(solution)/shard_map/ppermute | solution.py:63
  36.5 3.0 %collective-permute-start.11 = (bf16[8,32,512]{2,1,0:T(8,128)(2,1)}, bf16[8,32,512]{2,1,0:T(8,128)(2,1)S(1)}, u32[]{:S(2)}, u32[]{:S(2)}) collective-permute-start(bf16[8,32,512]{2,1,0:T(8,128)(2,1)} %get-tuple-element.50), channel_id=1, source_target_pairs={{0,2},{1,7},{2,0},{3,5},{4,6},{5,3},{6,4},{7,1},{8,10},{9,15},{10,... | collective-permute-start | bytes 786440 | tf_op jit(solution)/shard_map/ppermute | solution.py:63
  39.5 1.9 constant_dynamic-update-slice_fusion.21
  44.9 2.7 %collective-permute-start.14 = (bf16[16,16,1024]{2,1,0:T(8,128)(2,1)S(1)}, bf16[16,16,1024]{2,1,0:T(8,128)(2,1)S(1)}, u32[]{:S(2)}, u32[]{:S(2)}) collective-permute-start(bf16[16,16,1024]{2,1,0:T(8,128)(2,1)S(1)} %pad_maximum_fusion.5), channel_id=1, source_target_pairs={{0,8},{1,25},{2,10},{3,27},{4,12},{5,29},{6,14},{7,31},{8,0},{9,17... | collective-permute-start | bytes 1572872 | tf_op jit(solution)/shard_map/ppermute | solution.py:63
  47.7 2.2 %collective-permute-done.7 = bf16[8,32,512]{2,1,0:T(8,128)(2,1)S(1)} collective-permute-done((bf16[8,32,512]{2,1,0:T(8,128)(2,1)S(1)}, bf16[8,32,512]{2,1,0:T(8,128)(2,1)S(1)}, u32[]{:S(2)}, u32[]{:S(2)}) %collective-permute-start.7) | collective-permute-done | bytes 262176 | tf_op jit(solution)/shard_map/ppermute | solution.py:63
  51.9 2.7 %collective-permute-start.10 = (bf16[16,32,512]{2,1,0:T(8,128)(2,1)S(1)}, bf16[16,32,512]{2,1,0:T(8,128)(2,1)S(1)}, u32[]{:S(2)}, u32[]{:S(2)}) collective-permute-start(bf16[16,32,512]{2,1,0:T(8,128)(2,1)S(1)} %pad_maximum_fusion.3), channel_id=1, source_target_pairs={{0,2},{1,7},{2,0},{3,5},{4,6},{5,3},{6,4},{7,1},{8,10},{9,15},{10,... | collective-permute-start | bytes 1572872 | tf_op jit(solution)/shard_map/ppermute | solution.py:63
  57.0 2.2 %collective-permute-done.12 = bf16[16,32,512]{2,1,0:T(8,128)(2,1)S(1)} collective-permute-done((bf16[16,32,512]{2,1,0:T(8,128)(2,1)S(1)}, bf16[16,32,512]{2,1,0:T(8,128)(2,1)S(1)}, u32[]{:S(2)}, u32[]{:S(2)}) %collective-permute-start.12) | collective-permute-done | bytes 524320 | tf_op jit(solution)/shard_map/ppermute | solution.py:63
  59.1 2.7 %collective-permute-start.16 = (bf16[16,16,1024]{2,1,0:T(8,128)(2,1)S(1)}, bf16[16,16,1024]{2,1,0:T(8,128)(2,1)S(1)}, u32[]{:S(2)}, u32[]{:S(2)}) collective-permute-start(bf16[16,16,1024]{2,1,0:T(8,128)(2,1)S(1)} %pad_maximum_fusion.6), channel_id=1, source_target_pairs={{0,2},{1,7},{2,0},{3,5},{4,6},{5,3},{6,4},{7,1},{8,10},{9,15},{10,... | collective-permute-start | bytes 1572872 | tf_op jit(solution)/shard_map/ppermute | solution.py:63
  63.4 2.7 %collective-permute-done.8 = bf16[16,32,512]{2,1,0:T(8,128)(2,1)S(1)} collective-permute-done((bf16[16,32,512]{2,1,0:T(8,128)(2,1)S(1)}, bf16[16,32,512]{2,1,0:T(8,128)(2,1)S(1)}, u32[]{:S(2)}, u32[]{:S(2)}) %collective-permute-start.8) | collective-permute-done | bytes 524320 | tf_op jit(solution)/shard_map/ppermute | solution.py:63
  66.1 1.5 collective-permute-start.19
  68.4 2.7 %collective-permute-start.18 = (bf16[32,32,512]{2,1,0:T(8,128)(2,1)S(1)}, bf16[32,32,512]{2,1,0:T(8,128)(2,1)S(1)}, u32[]{:S(2)}, u32[]{:S(2)}) collective-permute-start(bf16[32,32,512]{2,1,0:T(8,128)(2,1)S(1)} %constant_dynamic-update-slice_fusion.10.refs_5_), channel_id=1, source_target_pairs={{0,2},{1,7},{2,0},{3,5},{4,6},{5,3},{6,4},{7,1},{8,10},{9,15},{10,... | collective-permute-start | bytes 3145736 | tf_op jit(solution)/shard_map/ppermute | solution.py:63
  73.8 1.6 fusion.3.refs_2_
  75.4 2.3 %collective-permute-done.20.refs_10_ = bf16[32,32,512]{2,1,0:T(8,128)(2,1)S(1)} collective-permute-done((bf16[32,32,512]{2,1,0:T(8,128)(2,1)S(1)}, bf16[32,32,512]{2,1,0:T(8,128)(2,1)S(1)}, u32[]{:S(2)}, u32[]{:S(2)}) %collective-permute-start.20) | collective-permute-done | bytes 1048608 | tf_op jit(solution)/shard_map/ppermute | solution.py:63
  77.7 3.2 %collective-permute-done.19.refs_8_ = bf16[32,32,512]{2,1,0:T(8,128)(2,1)S(1)} collective-permute-done((bf16[32,32,512]{2,1,0:T(8,128)(2,1)S(1)}, bf16[32,32,512]{2,1,0:T(8,128)(2,1)S(1)}, u32[]{:S(2)}, u32[]{:S(2)}) %collective-permute-start.19) | collective-permute-done | bytes 1048608 | tf_op jit(solution)/shard_map/ppermute | solution.py:63
  80.9 2.3 %collective-permute-done.18.refs_6_ = bf16[32,32,512]{2,1,0:T(8,128)(2,1)S(1)} collective-permute-done((bf16[32,32,512]{2,1,0:T(8,128)(2,1)S(1)}, bf16[32,32,512]{2,1,0:T(8,128)(2,1)S(1)}, u32[]{:S(2)}, u32[]{:S(2)}) %collective-permute-start.18) | collective-permute-done | bytes 1048608 | tf_op jit(solution)/shard_map/ppermute | solution.py:63
  84.3 18.2 %project.1 = (bf16[2,768,512]{2,1,0:T(8,128)(2,1)}, bf16[4,768,128]{2,1,0:T(8,128)(2,1)}, bf16[2,768,512]{2,1,0:T(8,128)(2,1)}, bf16[32,16,1024]{2,1,0:T(8,128)(...) custom-call(s32[5,64]{1,0:T(8,128)} %pad_add_fusion.refs_0_, ...), custom_call_target="tpu_custom_call" | custom-call | flops 8053063680 | bytes 20971520 | tf_op jit(solution)/shard_map/project/pallas_call | solution.py:232
  103.7 2.7 %collective-permute-start.24 = (bf16[32,16,1024]{2,1,0:T(8,128)(2,1)}, bf16[32,16,1024]{2,1,0:T(8,128)(2,1)S(1)}, u32[]{:S(2)}, u32[]{:S(2)}) collective-permute-start(bf16[32,16,1024]{2,1,0:T(8,128)(2,1)} %get-tuple-element.58), channel_id=1, source_target_pairs={{0,2},{1,7},{2,0},{3,5},{4,6},{5,3},{6,4},{7,1},{8,10},{9,15},{10,... | collective-permute-start | bytes 3145736 | tf_op jit(solution)/shard_map/ppermute | solution.py:63
  106.4 24.8 %back.1 = (bf16[64,16,2048]{2,1,0:T(8,128)(2,1)}, bf16[32,32,512]{2,1,0:T(8,128)(2,1)}, bf16[32,32,512]{2,1,0:T(8,128)(2,1)}, bf16[32,32,512]{2,1,0:T(8,128)(2,1...) custom-call(s32[5,64]{1,0:T(8,128)} %pad_add_fusion.refs_0_, ...), custom_call_target="tpu_custom_call" | custom-call | flops 8053063680 | bytes 20971520 | tf_op jit(solution)/shard_map/back/pallas_call | solution.py:333
  134.7 1.9 fusion.5
  136.7 2.0 collective-permute-start.26
  139.7 1.5 collective-permute-start.33
  141.3 1.7 collective-permute-start.28
  142.9 8.7 %collective-permute-done.26 = bf16[32,32,512]{2,1,0:T(8,128)(2,1)S(1)} collective-permute-done((bf16[32,32,512]{2,1,0:T(8,128)(2,1)S(1)}, bf16[32,32,512]{2,1,0:T(8,128)(2,1)S(1)}, u32[]{:S(2)}, u32[]{:S(2)}) %collective-permute-start.26) | collective-permute-done | bytes 1048608 | tf_op jit(solution)/shard_map/ppermute | solution.py:63
  151.7 1.9 collective-permute-start.27
  154.1 1.6 collective-permute-start.36
  157.4 3.5 %collective-permute-done.27 = bf16[16,16,1024]{2,1,0:T(8,128)(2,1)S(1)} collective-permute-done((bf16[16,16,1024]{2,1,0:T(8,128)(2,1)S(1)}, bf16[16,16,1024]{2,1,0:T(8,128)(2,1)S(1)}, u32[]{:S(2)}, u32[]{:S(2)}) %collective-permute-start.27) | collective-permute-done | bytes 524320 | tf_op jit(solution)/shard_map/ppermute | solution.py:63
  160.9 1.8 collective-permute-start.34
  163.0 1.6 collective-permute-start.38
  166.2 3.0 %add_convert_fusion = bf16[384,2048]{1,0:T(8,128)(2,1)} fusion(f32[384,2048]{1,0:T(8,128)S(1)} %collective-permute-done.29, bf16[384,1024]{1,0:T(8,128)(2,1)S(1)} %fusion.4, bf16[1024,2048]{1,0:T(8,128)(2,1)S(1)} %bitcast.92), kind=kOutput, calls=%fused_computation.8 | convolution fusion | flops 1612185600 | bytes 9699328 | tf_op jit(solution)/shard_map/dot_general | solution.py:509
  169.2 1.8 collective-permute-start.37
  172.3 1.6 collective-permute-start.32
  174.1 4.8 %collective-permute-done.32 = bf16[8,32,512]{2,1,0:T(8,128)(2,1)S(1)} collective-permute-done((bf16[8,32,512]{2,1,0:T(8,128)(2,1)S(1)}, bf16[8,32,512]{2,1,0:T(8,128)(2,1)S(1)}, u32[]{:S(2)}, u32[]{:S(2)}) %collective-permute-start.32) | collective-permute-done | bytes 262176 | tf_op jit(solution)/shard_map/ppermute | solution.py:63
  180.4 1.7 collective-permute-start.41
  182.1 4.5 %collective-permute-done.40 = bf16[2,160,512]{2,1,0:T(8,128)(2,1)S(1)} collective-permute-done((bf16[2,160,512]{2,1,0:T(8,128)(2,1)S(1)}, bf16[2,160,512]{2,1,0:T(8,128)(2,1)S(1)}, u32[]{:S(2)}, u32[]{:S(2)}) %collective-permute-start.40) | collective-permute-done | bytes 327712 | tf_op jit(solution)/shard_map/ppermute | solution.py:63
  186.6 2.7 %collective-permute-done.42 = bf16[2,160,512]{2,1,0:T(8,128)(2,1)S(1)} collective-permute-done((bf16[2,160,512]{2,1,0:T(8,128)(2,1)S(1)}, bf16[2,160,512]{2,1,0:T(8,128)(2,1)S(1)}, u32[]{:S(2)}, u32[]{:S(2)}) %collective-permute-start.42) | collective-permute-done | bytes 327712 | tf_op jit(solution)/shard_map/ppermute | solution.py:63
  190.1 4.2 %collective-permute-done.43 = bf16[160,512]{1,0:T(8,128)(2,1)S(1)} collective-permute-done((bf16[160,512]{1,0:T(8,128)(2,1)S(1)}, bf16[160,512]{1,0:T(8,128)(2,1)S(1)}, u32[]{:S(2)}, u32[]{:S(2)}) %collective-permute-start.43) | collective-permute-done | bytes 163872 | tf_op jit(solution)/shard_map/ppermute | solution.py:63
  195.1 11.0 %all-to-all-start = ((f32[128,1,128]{2,1,0:T(1,128)}), f32[128,1,128]{2,1,0:T(1,128)S(1)}, u32[]{:S(2)}, u32[]{:S(2)}) async-start(f32[128,1,128]{2,1,0:T(1,128)} %broadcast_in_dim.2), calls=%async_computation | async-start | bytes 131072 | tf_op jit(solution)/shard_map/all_to_all | solution.py:524
  207.3 4.1 %collective-permute-start.45 = (f32[16,2048]{1,0:T(8,128)S(1)}, f32[16,2048]{1,0:T(8,128)S(1)}, u32[]{:S(2)}, u32[]{:S(2)}) collective-permute-start(f32[16,2048]{1,0:T(8,128)S(1)} %pad_maximum_fusion.8), channel_id=1, source_target_pairs={{0,0},{32,1},{2,2},{34,3},{4,4},{36,5},{6,6},{38,7},{8,8},{40,9},{... | collective-permute-start | bytes 393224 | tf_op jit(solution)/shard_map/ppermute | solution.py:539
  211.4 4.0 %all-to-all-done = f32[128,1,128]{2,1,0:T(1,128)S(1)} async-done(((f32[128,1,128]{2,1,0:T(1,128)}), f32[128,1,128]{2,1,0:T(1,128)S(1)}, u32[]{:S(2)}, u32[]{:S(2)}) %all-to-all-start) | async-done | bytes 65568 | tf_op jit(solution)/shard_map/all_to_all | solution.py:524
  (209 shorter events, 38.7 us)
Async XLA Ops:
  1.7 9.0 %collective-permute-start.2 = (bf16[16,2048]{1,0:T(8,128)(2,1)S(1)}, bf16[16,2048]{1,0:T(8,128)(2,1)S(1)}, u32[]{:S(2)}, u32[]{:S(2)}) collective-permute-start(bf16[16,2048]{1,0:T(8,128)(2,1)S(1)} %convert_element_type.270), channel_id=1, source_target_pairs={{0,0},{1,32},{2,2},{3,34},{4,4},{5,36},{6,6},{7,38},{8,8},{9,40},{... | collective-permute-start | bytes 196616 | tf_op jit(solution)/shard_map/ppermute | solution.py:460
  7.2 3.4 %collective-permute-start = (bf16[16,1536]{1,0:T(8,128)(2,1)S(1)}, bf16[16,1536]{1,0:T(8,128)(2,1)S(1)}, u32[]{:S(2)}, u32[]{:S(2)}) collective-permute-start(bf16[16,1536]{1,0:T(8,128)(2,1)S(1)} %broadcast_select_fusion.3), channel_id=1, source_target_pairs={{0,1},{1,0},{2,3},{3,2},{4,5},{5,4},{6,7},{7,6},{8,9},{9,8},{10,11... | collective-permute-start | bytes 147464 | tf_op jit(solution)/shard_map/ppermute | solution.py:71
  10.7 4.6 %collective-permute-start.3 = (bf16[160,512]{1,0:T(8,128)(2,1)S(1)}, bf16[160,512]{1,0:T(8,128)(2,1)S(1)}, u32[]{:S(2)}, u32[]{:S(2)}) collective-permute-start(bf16[160,512]{1,0:T(8,128)(2,1)S(1)} %constant_dynamic-update-slice_fusion), channel_id=1, source_target_pairs={{0,96},{1,33},{2,98},{3,35},{4,100},{5,37},{6,102},{7,39},{8,104},... | collective-permute-start | bytes 491528 | tf_op jit(solution)/shard_map/ppermute | solution.py:63
  15.4 12.5 %collective-permute-start.6 = (bf16[2,160,512]{2,1,0:T(8,128)(2,1)S(1)}, bf16[2,160,512]{2,1,0:T(8,128)(2,1)}, u32[]{:S(2)}, u32[]{:S(2)}) collective-permute-start(bf16[2,160,512]{2,1,0:T(8,128)(2,1)S(1)} %pad_maximum_fusion.7.refs_0_), channel_id=1, source_target_pairs={{0,30},{1,11},{2,28},{3,9},{4,26},{5,15},{6,24},{7,13},{8,22},{9,3... | collective-permute-start | bytes 983048 | tf_op jit(solution)/shard_map/ppermute | solution.py:63
  18.2 9.8 %collective-permute-start.5 = (bf16[2,160,512]{2,1,0:T(8,128)(2,1)S(1)}, bf16[2,160,512]{2,1,0:T(8,128)(2,1)}, u32[]{:S(2)}, u32[]{:S(2)}) collective-permute-start(bf16[2,160,512]{2,1,0:T(8,128)(2,1)S(1)} %pad_maximum_fusion.7.refs_0_), channel_id=1, source_target_pairs={{0,6},{1,3},{2,4},{3,1},{4,2},{5,7},{6,0},{7,5},{8,14},{9,11},{10,... | collective-permute-start | bytes 983048 | tf_op jit(solution)/shard_map/ppermute | solution.py:63
  18.2 9.8 %collective-permute-start.4 = (bf16[2,160,512]{2,1,0:T(8,128)(2,1)S(1)}, bf16[2,160,512]{2,1,0:T(8,128)(2,1)}, u32[]{:S(2)}, u32[]{:S(2)}) collective-permute-start(bf16[2,160,512]{2,1,0:T(8,128)(2,1)S(1)} %pad_maximum_fusion.7.refs_0_), channel_id=1, source_target_pairs={{0,24},{1,9},{2,26},{3,11},{4,28},{5,13},{6,30},{7,15},{8,16},{9,1... | collective-permute-start | bytes 983048 | tf_op jit(solution)/shard_map/ppermute | solution.py:63
  18.5 7.5 %collective-permute-start.21 = (s32[384]{0:T(512)S(1)}, s32[384]{0:T(512)S(1)}, u32[]{:S(2)}, u32[]{:S(2)}) collective-permute-start(s32[384]{0:T(512)S(1)} %copy-done.24), channel_id=1, source_target_pairs={{0,1},{1,0},{2,3},{3,2},{4,5},{5,4},{6,7},{7,6},{8,9},{9,8},{10,11... | collective-permute-start | bytes 4616 | tf_op jit(solution)/shard_map/ppermute | solution.py:71
  25.8 46.2 %collective-permute-start.1 = (bf16[384,2048]{1,0:T(8,128)(2,1)S(1)}, bf16[384,2048]{1,0:T(8,128)(2,1)S(1)}, u32[]{:S(2)}, u32[]{:S(2)}) collective-permute-start(bf16[384,2048]{1,0:T(8,128)(2,1)S(1)} %copy-done), channel_id=1, source_target_pairs={{0,1},{1,0},{2,3},{3,2},{4,5},{5,4},{6,7},{7,6},{8,9},{9,8},{10,11... | collective-permute-start | bytes 4718600 | tf_op jit(solution)/shard_map/ppermute | solution.py:71
  26.0 47.5 %collective-permute-start.17 = (bf16[384,2048]{1,0:T(8,128)(2,1)}, bf16[384,2048]{1,0:T(8,128)(2,1)}, u32[]{:S(2)}, u32[]{:S(2)}) collective-permute-start(bf16[384,2048]{1,0:T(8,128)(2,1)} %refs_3_.3), channel_id=1, source_target_pairs={{0,1},{1,0},{2,3},{3,2},{4,5},{5,4},{6,7},{7,6},{8,9},{9,8},{10,11... | collective-permute-start | bytes 4718600 | tf_op jit(solution)/shard_map/ppermute | solution.py:71
  30.1 14.5 %collective-permute-start.13 = (bf16[8,16,1024]{2,1,0:T(8,128)(2,1)}, bf16[8,16,1024]{2,1,0:T(8,128)(2,1)S(1)}, u32[]{:S(2)}, u32[]{:S(2)}) collective-permute-start(bf16[8,16,1024]{2,1,0:T(8,128)(2,1)} %get-tuple-element.51), channel_id=1, source_target_pairs={{0,32},{1,97},{2,34},{3,99},{4,36},{5,101},{6,38},{7,103},{8,40},{... | collective-permute-start | bytes 786440 | tf_op jit(solution)/shard_map/ppermute | solution.py:63
  34.2 10.8 %collective-permute-start.9 = (bf16[8,32,512]{2,1,0:T(8,128)(2,1)}, bf16[8,32,512]{2,1,0:T(8,128)(2,1)S(1)}, u32[]{:S(2)}, u32[]{:S(2)}) collective-permute-start(bf16[8,32,512]{2,1,0:T(8,128)(2,1)} %get-tuple-element.49), channel_id=1, source_target_pairs={{0,8},{1,25},{2,10},{3,27},{4,12},{5,29},{6,14},{7,31},{8,0},{9,17... | collective-permute-start | bytes 786440 | tf_op jit(solution)/shard_map/ppermute | solution.py:63
  36.5 6.9 %collective-permute-start.11 = (bf16[8,32,512]{2,1,0:T(8,128)(2,1)}, bf16[8,32,512]{2,1,0:T(8,128)(2,1)S(1)}, u32[]{:S(2)}, u32[]{:S(2)}) collective-permute-start(bf16[8,32,512]{2,1,0:T(8,128)(2,1)} %get-tuple-element.50), channel_id=1, source_target_pairs={{0,2},{1,7},{2,0},{3,5},{4,6},{5,3},{6,4},{7,1},{8,10},{9,15},{10,... | collective-permute-start | bytes 786440 | tf_op jit(solution)/shard_map/ppermute | solution.py:63
  43.5 6.4 %collective-permute-start.7 = (bf16[8,32,512]{2,1,0:T(8,128)(2,1)S(1)}, bf16[8,32,512]{2,1,0:T(8,128)(2,1)S(1)}, u32[]{:S(2)}, u32[]{:S(2)}) collective-permute-start(bf16[8,32,512]{2,1,0:T(8,128)(2,1)S(1)} %copy-done.10), channel_id=1, source_target_pairs={{0,32},{1,97},{2,34},{3,99},{4,36},{5,101},{6,38},{7,103},{8,40},{... | collective-permute-start | bytes 786440 | tf_op jit(solution)/shard_map/ppermute | solution.py:63
  44.7 7.2 %collective-permute-start.15 = (bf16[8,16,1024]{2,1,0:T(8,128)(2,1)S(1)}, bf16[8,16,1024]{2,1,0:T(8,128)(2,1)S(1)}, u32[]{:S(2)}, u32[]{:S(2)}) collective-permute-start(bf16[8,16,1024]{2,1,0:T(8,128)(2,1)S(1)} %copy-done.9), channel_id=1, source_target_pairs={{0,8},{1,25},{2,10},{3,27},{4,12},{5,29},{6,14},{7,31},{8,0},{9,17... | collective-permute-start | bytes 786440 | tf_op jit(solution)/shard_map/ppermute | solution.py:63
  44.9 11.9 %collective-permute-start.14 = (bf16[16,16,1024]{2,1,0:T(8,128)(2,1)S(1)}, bf16[16,16,1024]{2,1,0:T(8,128)(2,1)S(1)}, u32[]{:S(2)}, u32[]{:S(2)}) collective-permute-start(bf16[16,16,1024]{2,1,0:T(8,128)(2,1)S(1)} %pad_maximum_fusion.5), channel_id=1, source_target_pairs={{0,8},{1,25},{2,10},{3,27},{4,12},{5,29},{6,14},{7,31},{8,0},{9,17... | collective-permute-start | bytes 1572872 | tf_op jit(solution)/shard_map/ppermute | solution.py:63
  49.9 9.2 %collective-permute-start.12 = (bf16[16,32,512]{2,1,0:T(8,128)(2,1)S(1)}, bf16[16,32,512]{2,1,0:T(8,128)(2,1)S(1)}, u32[]{:S(2)}, u32[]{:S(2)}) collective-permute-start(bf16[16,32,512]{2,1,0:T(8,128)(2,1)S(1)} %pad_maximum_fusion.4), channel_id=1, source_target_pairs={{0,32},{1,97},{2,34},{3,99},{4,36},{5,101},{6,38},{7,103},{8,40},{... | collective-permute-start | bytes 1572872 | tf_op jit(solution)/shard_map/ppermute | solution.py:63
  51.9 11.0 %collective-permute-start.10 = (bf16[16,32,512]{2,1,0:T(8,128)(2,1)S(1)}, bf16[16,32,512]{2,1,0:T(8,128)(2,1)S(1)}, u32[]{:S(2)}, u32[]{:S(2)}) collective-permute-start(bf16[16,32,512]{2,1,0:T(8,128)(2,1)S(1)} %pad_maximum_fusion.3), channel_id=1, source_target_pairs={{0,2},{1,7},{2,0},{3,5},{4,6},{5,3},{6,4},{7,1},{8,10},{9,15},{10,... | collective-permute-start | bytes 1572872 | tf_op jit(solution)/shard_map/ppermute | solution.py:63
  56.8 9.2 %collective-permute-start.8 = (bf16[16,32,512]{2,1,0:T(8,128)(2,1)S(1)}, bf16[16,32,512]{2,1,0:T(8,128)(2,1)S(1)}, u32[]{:S(2)}, u32[]{:S(2)}) collective-permute-start(bf16[16,32,512]{2,1,0:T(8,128)(2,1)S(1)} %pad_maximum_fusion.2), channel_id=1, source_target_pairs={{0,8},{1,25},{2,10},{3,27},{4,12},{5,29},{6,14},{7,31},{8,0},{9,17... | collective-permute-start | bytes 1572872 | tf_op jit(solution)/shard_map/ppermute | solution.py:63
  59.1 9.2 %collective-permute-start.16 = (bf16[16,16,1024]{2,1,0:T(8,128)(2,1)S(1)}, bf16[16,16,1024]{2,1,0:T(8,128)(2,1)S(1)}, u32[]{:S(2)}, u32[]{:S(2)}) collective-permute-start(bf16[16,16,1024]{2,1,0:T(8,128)(2,1)S(1)} %pad_maximum_fusion.6), channel_id=1, source_target_pairs={{0,2},{1,7},{2,0},{3,5},{4,6},{5,3},{6,4},{7,1},{8,10},{9,15},{10,... | collective-permute-start | bytes 1572872 | tf_op jit(solution)/shard_map/ppermute | solution.py:63
  62.8 14.9 %collective-permute-start.20 = (bf16[32,32,512]{2,1,0:T(8,128)(2,1)S(1)}, bf16[32,32,512]{2,1,0:T(8,128)(2,1)S(1)}, u32[]{:S(2)}, u32[]{:S(2)}) collective-permute-start(bf16[32,32,512]{2,1,0:T(8,128)(2,1)S(1)} %constant_dynamic-update-slice_fusion.16.refs_9_), channel_id=1, source_target_pairs={{0,8},{1,25},{2,10},{3,27},{4,12},{5,29},{6,14},{7,31},{8,0},{9,17... | collective-permute-start | bytes 3145736 | tf_op jit(solution)/shard_map/ppermute | solution.py:63
  66.1 14.9 %collective-permute-start.19 = (bf16[32,32,512]{2,1,0:T(8,128)(2,1)S(1)}, bf16[32,32,512]{2,1,0:T(8,128)(2,1)S(1)}, u32[]{:S(2)}, u32[]{:S(2)}) collective-permute-start(bf16[32,32,512]{2,1,0:T(8,128)(2,1)S(1)} %constant_dynamic-update-slice_fusion.13.refs_7_), channel_id=1, source_target_pairs={{0,32},{1,97},{2,34},{3,99},{4,36},{5,101},{6,38},{7,103},{8,40},{... | collective-permute-start | bytes 3145736 | tf_op jit(solution)/shard_map/ppermute | solution.py:63
  68.4 14.9 %collective-permute-start.18 = (bf16[32,32,512]{2,1,0:T(8,128)(2,1)S(1)}, bf16[32,32,512]{2,1,0:T(8,128)(2,1)S(1)}, u32[]{:S(2)}, u32[]{:S(2)}) collective-permute-start(bf16[32,32,512]{2,1,0:T(8,128)(2,1)S(1)} %constant_dynamic-update-slice_fusion.10.refs_5_), channel_id=1, source_target_pairs={{0,2},{1,7},{2,0},{3,5},{4,6},{5,3},{6,4},{7,1},{8,10},{9,15},{10,... | collective-permute-start | bytes 3145736 | tf_op jit(solution)/shard_map/ppermute | solution.py:63
  72.0 34.4 %collective-permute-start.23 = (bf16[32,16,1024]{2,1,0:T(8,128)(2,1)}, bf16[32,16,1024]{2,1,0:T(8,128)(2,1)}, u32[]{:S(2)}, u32[]{:S(2)}) collective-permute-start(bf16[32,16,1024]{2,1,0:T(8,128)(2,1)} %constant_dynamic-update-slice_fusion.22.refs_7_), channel_id=1, source_target_pairs={{0,32},{1,97},{2,34},{3,99},{4,36},{5,101},{6,38},{7,103},{8,40},{... | collective-permute-start | bytes 3145736 | tf_op jit(solution)/shard_map/ppermute | solution.py:63
  73.5 32.9 %collective-permute-start.22 = (bf16[32,16,1024]{2,1,0:T(8,128)(2,1)}, bf16[32,16,1024]{2,1,0:T(8,128)(2,1)}, u32[]{:S(2)}, u32[]{:S(2)}) collective-permute-start(bf16[32,16,1024]{2,1,0:T(8,128)(2,1)} %constant_dynamic-update-slice_fusion.19.refs_5_), channel_id=1, source_target_pairs={{0,2},{1,7},{2,0},{3,5},{4,6},{5,3},{6,4},{7,1},{8,10},{9,15},{10,... | collective-permute-start | bytes 3145736 | tf_op jit(solution)/shard_map/ppermute | solution.py:63
  102.5 28.7 %collective-permute-start.25 = (bf16[32,16,1024]{2,1,0:T(8,128)(2,1)}, bf16[32,16,1024]{2,1,0:T(8,128)(2,1)S(1)}, u32[]{:S(2)}, u32[]{:S(2)}) collective-permute-start(bf16[32,16,1024]{2,1,0:T(8,128)(2,1)} %get-tuple-element.68), channel_id=1, source_target_pairs={{0,32},{1,97},{2,34},{3,99},{4,36},{5,101},{6,38},{7,103},{8,40},{... | collective-permute-start | bytes 3145736 | tf_op jit(solution)/shard_map/ppermute | solution.py:63
  103.7 27.9 %collective-permute-start.24 = (bf16[32,16,1024]{2,1,0:T(8,128)(2,1)}, bf16[32,16,1024]{2,1,0:T(8,128)(2,1)S(1)}, u32[]{:S(2)}, u32[]{:S(2)}) collective-permute-start(bf16[32,16,1024]{2,1,0:T(8,128)(2,1)} %get-tuple-element.58), channel_id=1, source_target_pairs={{0,2},{1,7},{2,0},{3,5},{4,6},{5,3},{6,4},{7,1},{8,10},{9,15},{10,... | collective-permute-start | bytes 3145736 | tf_op jit(solution)/shard_map/ppermute | solution.py:63
  136.6 28.1 %collective-permute-start.29 = (f32[384,2048]{1,0:T(8,128)S(1)}, f32[384,2048]{1,0:T(8,128)S(1)}, u32[]{:S(2)}, u32[]{:S(2)}) collective-permute-start(f32[384,2048]{1,0:T(8,128)S(1)} %fusion.5), channel_id=1, source_target_pairs={{0,1},{1,0},{2,3},{3,2},{4,5},{5,4},{6,7},{7,6},{8,9},{9,8},{10,11... | collective-permute-start | bytes 9437192 | tf_op jit(solution)/shard_map/ppermute | solution.py:71
  136.7 14.9 %collective-permute-start.26 = (bf16[32,32,512]{2,1,0:T(8,128)(2,1)S(1)}, bf16[32,32,512]{2,1,0:T(8,128)(2,1)S(1)}, u32[]{:S(2)}, u32[]{:S(2)}) collective-permute-start(bf16[32,32,512]{2,1,0:T(8,128)(2,1)S(1)} %copy-done.27), channel_id=1, source_target_pairs={{0,8},{1,25},{2,10},{3,27},{4,12},{5,29},{6,14},{7,31},{8,0},{9,17... | collective-permute-start | bytes 3145736 | tf_op jit(solution)/shard_map/ppermute | solution.py:63
  138.7 15.4 %collective-permute-start.30 = (bf16[32,32,512]{2,1,0:T(8,128)(2,1)S(1)}, bf16[32,32,512]{2,1,0:T(8,128)(2,1)S(1)}, u32[]{:S(2)}, u32[]{:S(2)}) collective-permute-start(bf16[32,32,512]{2,1,0:T(8,128)(2,1)S(1)} %copy-done.26), channel_id=1, source_target_pairs={{0,2},{1,7},{2,0},{3,5},{4,6},{5,3},{6,4},{7,1},{8,10},{9,15},{10,... | collective-permute-start | bytes 3145736 | tf_op jit(solution)/shard_map/ppermute | solution.py:63
  139.7 16.4 %collective-permute-start.33 = (bf16[32,32,512]{2,1,0:T(8,128)(2,1)S(1)}, bf16[32,32,512]{2,1,0:T(8,128)(2,1)S(1)}, u32[]{:S(2)}, u32[]{:S(2)}) collective-permute-start(bf16[32,32,512]{2,1,0:T(8,128)(2,1)S(1)} %copy-done.25), channel_id=1, source_target_pairs={{0,32},{1,97},{2,34},{3,99},{4,36},{5,101},{6,38},{7,103},{8,40},{... | collective-permute-start | bytes 3145736 | tf_op jit(solution)/shard_map/ppermute | solution.py:63
  141.3 21.7 %collective-permute-start.28 = (bf16[16,16,1024]{2,1,0:T(8,128)(2,1)S(1)}, bf16[16,16,1024]{2,1,0:T(8,128)(2,1)S(1)}, u32[]{:S(2)}, u32[]{:S(2)}) collective-permute-start(bf16[16,16,1024]{2,1,0:T(8,128)(2,1)S(1)} %get-tuple-element.102), channel_id=1, source_target_pairs={{0,2},{1,7},{2,0},{3,5},{4,6},{5,3},{6,4},{7,1},{8,10},{9,15},{10,... | collective-permute-start | bytes 1572872 | tf_op jit(solution)/shard_map/ppermute | solution.py:63
  151.7 9.2 %collective-permute-start.27 = (bf16[16,16,1024]{2,1,0:T(8,128)(2,1)S(1)}, bf16[16,16,1024]{2,1,0:T(8,128)(2,1)S(1)}, u32[]{:S(2)}, u32[]{:S(2)}) collective-permute-start(bf16[16,16,1024]{2,1,0:T(8,128)(2,1)S(1)} %get-tuple-element.104), channel_id=1, source_target_pairs={{0,8},{1,25},{2,10},{3,27},{4,12},{5,29},{6,14},{7,31},{8,0},{9,17... | collective-permute-start | bytes 1572872 | tf_op jit(solution)/shard_map/ppermute | solution.py:63
  154.1 15.0 %collective-permute-start.36 = (bf16[16,32,512]{2,1,0:T(8,128)(2,1)S(1)}, bf16[16,32,512]{2,1,0:T(8,128)(2,1)S(1)}, u32[]{:S(2)}, u32[]{:S(2)}) collective-permute-start(bf16[16,32,512]{2,1,0:T(8,128)(2,1)S(1)} %get-tuple-element.96), channel_id=1, source_target_pairs={{0,32},{1,97},{2,34},{3,99},{4,36},{5,101},{6,38},{7,103},{8,40},{... | collective-permute-start | bytes 1572872 | tf_op jit(solution)/shard_map/ppermute | solution.py:63
  156.1 16.1 %collective-permute-start.31 = (bf16[16,32,512]{2,1,0:T(8,128)(2,1)S(1)}, bf16[16,32,512]{2,1,0:T(8,128)(2,1)S(1)}, u32[]{:S(2)}, u32[]{:S(2)}) collective-permute-start(bf16[16,32,512]{2,1,0:T(8,128)(2,1)S(1)} %get-tuple-element.100), channel_id=1, source_target_pairs={{0,8},{1,25},{2,10},{3,27},{4,12},{5,29},{6,14},{7,31},{8,0},{9,17... | collective-permute-start | bytes 1572872 | tf_op jit(solution)/shard_map/ppermute | solution.py:63
  160.9 10.1 %collective-permute-start.34 = (bf16[16,32,512]{2,1,0:T(8,128)(2,1)S(1)}, bf16[16,32,512]{2,1,0:T(8,128)(2,1)S(1)}, u32[]{:S(2)}, u32[]{:S(2)}) collective-permute-start(bf16[16,32,512]{2,1,0:T(8,128)(2,1)S(1)} %get-tuple-element.98), channel_id=1, source_target_pairs={{0,2},{1,7},{2,0},{3,5},{4,6},{5,3},{6,4},{7,1},{8,10},{9,15},{10,... | collective-permute-start | bytes 1572872 | tf_op jit(solution)/shard_map/ppermute | solution.py:63
  163.0 11.0 %collective-permute-start.38 = (bf16[8,16,1024]{2,1,0:T(8,128)(2,1)S(1)}, bf16[8,16,1024]{2,1,0:T(8,128)(2,1)S(1)}, u32[]{:S(2)}, u32[]{:S(2)}) collective-permute-start(bf16[8,16,1024]{2,1,0:T(8,128)(2,1)S(1)} %get-tuple-element.113), channel_id=1, source_target_pairs={{0,32},{1,97},{2,34},{3,99},{4,36},{5,101},{6,38},{7,103},{8,40},{... | collective-permute-start | bytes 786440 | tf_op jit(solution)/shard_map/ppermute | solution.py:63
  164.8 9.2 %collective-permute-start.39 = (bf16[8,16,1024]{2,1,0:T(8,128)(2,1)S(1)}, bf16[8,16,1024]{2,1,0:T(8,128)(2,1)S(1)}, u32[]{:S(2)}, u32[]{:S(2)}) collective-permute-start(bf16[8,16,1024]{2,1,0:T(8,128)(2,1)S(1)} %get-tuple-element.111), channel_id=1, source_target_pairs={{0,8},{1,25},{2,10},{3,27},{4,12},{5,29},{6,14},{7,31},{8,0},{9,17... | collective-permute-start | bytes 786440 | tf_op jit(solution)/shard_map/ppermute | solution.py:63
  169.2 9.9 %collective-permute-start.37 = (bf16[8,32,512]{2,1,0:T(8,128)(2,1)S(1)}, bf16[8,32,512]{2,1,0:T(8,128)(2,1)S(1)}, u32[]{:S(2)}, u32[]{:S(2)}) collective-permute-start(bf16[8,32,512]{2,1,0:T(8,128)(2,1)S(1)} %add_convert_fusion.16), channel_id=1, source_target_pairs={{0,2},{1,7},{2,0},{3,5},{4,6},{5,3},{6,4},{7,1},{8,10},{9,15},{10,... | collective-permute-start | bytes 786440 | tf_op jit(solution)/shard_map/ppermute | solution.py:63
  171.0 7.9 %collective-permute-start.35 = (bf16[8,32,512]{2,1,0:T(8,128)(2,1)S(1)}, bf16[8,32,512]{2,1,0:T(8,128)(2,1)S(1)}, u32[]{:S(2)}, u32[]{:S(2)}) collective-permute-start(bf16[8,32,512]{2,1,0:T(8,128)(2,1)S(1)} %add_convert_fusion.19), channel_id=1, source_target_pairs={{0,8},{1,25},{2,10},{3,27},{4,12},{5,29},{6,14},{7,31},{8,0},{9,17... | collective-permute-start | bytes 786440 | tf_op jit(solution)/shard_map/ppermute | solution.py:63
  172.3 6.5 %collective-permute-start.32 = (bf16[8,32,512]{2,1,0:T(8,128)(2,1)S(1)}, bf16[8,32,512]{2,1,0:T(8,128)(2,1)S(1)}, u32[]{:S(2)}, u32[]{:S(2)}) collective-permute-start(bf16[8,32,512]{2,1,0:T(8,128)(2,1)S(1)} %add_convert_fusion.22), channel_id=1, source_target_pairs={{0,32},{1,97},{2,34},{3,99},{4,36},{5,101},{6,38},{7,103},{8,40},{... | collective-permute-start | bytes 786440 | tf_op jit(solution)/shard_map/ppermute | solution.py:63
  179.4 7.2 %collective-permute-start.40 = (bf16[2,160,512]{2,1,0:T(8,128)(2,1)S(1)}, bf16[2,160,512]{2,1,0:T(8,128)(2,1)S(1)}, u32[]{:S(2)}, u32[]{:S(2)}) collective-permute-start(bf16[2,160,512]{2,1,0:T(8,128)(2,1)S(1)} %get-tuple-element.107), channel_id=1, source_target_pairs={{0,30},{1,11},{2,28},{3,9},{4,26},{5,15},{6,24},{7,13},{8,22},{9,3... | collective-permute-start | bytes 983048 | tf_op jit(solution)/shard_map/ppermute | solution.py:63
  179.5 9.8 %collective-permute-start.42 = (bf16[2,160,512]{2,1,0:T(8,128)(2,1)S(1)}, bf16[2,160,512]{2,1,0:T(8,128)(2,1)S(1)}, u32[]{:S(2)}, u32[]{:S(2)}) collective-permute-start(bf16[2,160,512]{2,1,0:T(8,128)(2,1)S(1)} %get-tuple-element.108), channel_id=1, source_target_pairs={{0,6},{1,3},{2,4},{3,1},{4,2},{5,7},{6,0},{7,5},{8,14},{9,11},{10,... | collective-permute-start | bytes 983048 | tf_op jit(solution)/shard_map/ppermute | solution.py:63
  180.4 9.4 %collective-permute-start.41 = (bf16[2,160,512]{2,1,0:T(8,128)(2,1)S(1)}, bf16[2,160,512]{2,1,0:T(8,128)(2,1)S(1)}, u32[]{:S(2)}, u32[]{:S(2)}) collective-permute-start(bf16[2,160,512]{2,1,0:T(8,128)(2,1)S(1)} %get-tuple-element.109), channel_id=1, source_target_pairs={{0,24},{1,9},{2,26},{3,11},{4,28},{5,13},{6,30},{7,15},{8,16},{9,1... | collective-permute-start | bytes 983048 | tf_op jit(solution)/shard_map/ppermute | solution.py:63
  190.0 26.9 %copy-start.13 = (f32[16,3072]{1,0:T(8,128)S(1)}, f32[16,3072]{1,0:T(8,128)}, u32[]{:S(2)}) copy-start(f32[16,3072]{1,0:T(8,128)} %param.14) | copy-start | bytes 589828
  190.0 4.2 %collective-permute-start.43 = (bf16[160,512]{1,0:T(8,128)(2,1)S(1)}, bf16[160,512]{1,0:T(8,128)(2,1)S(1)}, u32[]{:S(2)}, u32[]{:S(2)}) collective-permute-start(bf16[160,512]{1,0:T(8,128)(2,1)S(1)} %fusion.12), channel_id=1, source_target_pairs={{0,96},{1,33},{2,98},{3,35},{4,100},{5,37},{6,102},{7,39},{8,104},... | collective-permute-start | bytes 491528 | tf_op jit(solution)/shard_map/ppermute | solution.py:63
  195.1 20.3 %all-to-all-start = ((f32[128,1,128]{2,1,0:T(1,128)}), f32[128,1,128]{2,1,0:T(1,128)S(1)}, u32[]{:S(2)}, u32[]{:S(2)}) async-start(f32[128,1,128]{2,1,0:T(1,128)} %broadcast_in_dim.2), calls=%async_computation | async-start | bytes 131072 | tf_op jit(solution)/shard_map/all_to_all | solution.py:524
  206.1 10.6 %collective-permute-start.44 = (f32[3,16,512]{2,1,0:T(8,128)S(1)}, f32[3,16,512]{2,1,0:T(8,128)S(1)}, u32[]{:S(2)}, u32[]{:S(2)}) collective-permute-start(f32[3,16,512]{2,1,0:T(8,128)S(1)} %select_bitcast_fusion), channel_id=1, source_target_pairs={{0,1},{1,0},{2,3},{3,2},{4,5},{5,4},{6,7},{7,6},{8,9},{9,8},{10,11... | collective-permute-start | bytes 294920 | tf_op jit(solution)/shard_map/ppermute | solution.py:71
  207.3 10.5 %collective-permute-start.45 = (f32[16,2048]{1,0:T(8,128)S(1)}, f32[16,2048]{1,0:T(8,128)S(1)}, u32[]{:S(2)}, u32[]{:S(2)}) collective-permute-start(f32[16,2048]{1,0:T(8,128)S(1)} %pad_maximum_fusion.8), channel_id=1, source_target_pairs={{0,0},{32,1},{2,2},{34,3},{4,4},{36,5},{6,6},{38,7},{8,8},{40,9},{... | collective-permute-start | bytes 393224 | tf_op jit(solution)/shard_map/ppermute | solution.py:539
  (31 other events, 289.4 us)
